TPU v7x, 128 devices: a whole 4x4x4 slice. The times are simulated.
128 devices in a mesh: dp: 32 (over x, z_hi, y), expert: 4 (over z_lo, core).
Axes of the slice: x: 4, y: 4, z: 4 (z_hi: 2, z_lo: 2; z = z_hi * 2 + z_lo), core: 2. Of those that a mesh axis runs over, the one named last changes fastest.
Arguments:
- tokens: bfloat16 [16384, 2048], P(('dp', 'expert')), may hold values from -6 to 6
- cotangent: bfloat16 [16384, 2048], P(('dp', 'expert')), may hold values from -6 to 6
- expert_ids: int32 [16384, 2], P(('dp', 'expert')), may hold values from 0 to 3, all different within a row; in each aligned block of 128 rows (0 to 127, 128 to 255, ...) at most 128 rows name the same one
- combine: float32 [16384, 2], P(('dp', 'expert')), may hold values from 0.1 to 1
- w_gate: bfloat16 [4, 2048, 768], P('expert'), may hold values from -0.125 to 0.125
- w_up: bfloat16 [4, 2048, 768], P('expert'), may hold values from -0.125 to 0.125
- w_down: bfloat16 [4, 768, 2048], P('expert'), may hold values from -0.21875 to 0.21875
Outputs:
- input_grad: bfloat16 [16384, 2048], P(('dp', 'expert'))
- combine_grad: float32 [16384, 2], P(('dp', 'expert'))
- gate_grad: bfloat16 [4, 2048, 768], P('expert', 'dp')
- up_grad: bfloat16 [4, 2048, 768], P('expert', 'dp')
- down_grad: bfloat16 [4, 768, 2048], P('expert', 'dp')
Inputs may be any that keep to these rules, and one draw needn't show every extreme that they name: `expert_ids`: each token names 2 different experts. In the rows of one device no expert is named by more than 128 tokens, and in some devices' rows some expert is named by exactly 128.
All inputs are finite; a program needn't handle non-finite values.
Results may differ from a plain program's by a relative error of at most 0.02.
Values may be sent and summed in bfloat16 or wider, within the bound.
A program may use at most 128 MiB of HBM per device.

v0:
```python
import jax
import jax.numpy as jnp
from jax import lax
from jax.sharding import Mesh
from jax.sharding import PartitionSpec as P

EXPERT = ("expert_0", "expert_1")
DP_EXPERT = ("dp", "expert_0", "expert_1")


def cut_along(array, dim, length):
    before, after = (array.shape[:dim], array.shape[dim + 1 :])
    return jnp.moveaxis(array.reshape(*before, length, -1, *after), dim, 0)


def one_scatter(arrays, axis, dims):
    length = lax.axis_size(axis)
    blocks = [cut_along(a, dim, length) for a, dim in zip(arrays, dims)]
    lines = jnp.concatenate([b.reshape(length, -1) for b in blocks], axis=1)
    extent = max(16, -(-lines.shape[1] // 1024) * 8)
    lines = jnp.pad(lines, ((0, 0), (0, extent * 128 - lines.shape[1]))).reshape(-1, 128)
    ravelled, at, outs = (lax.psum_scatter(lines, axis, tiled=True).reshape(-1), 0, [])
    for b in blocks:
        part = b[0]
        outs.append(ravelled[at : at + part.size].reshape(part.shape))
        at += part.size
    return tuple(outs)


def laid_out(blocks, dim):
    lengths = list(blocks.shape[1:])
    lengths[dim] *= blocks.shape[0]
    return jnp.moveaxis(blocks, 0, dim).reshape(lengths)


def moved_by_axis(blocks, axes, order):
    lengths = [lax.axis_size(a) for a in axes]
    blocks = blocks.reshape(*lengths, *blocks.shape[1:])
    for k in order:
        blocks = lax.all_to_all(blocks, axes[k], split_axis=k, concat_axis=k, tiled=True)
    return blocks.reshape(-1, *blocks.shape[len(axes) :])


def core_and_chips(array, groups, order, split_dim, concat_dim):
    length = lax.axis_size(groups[0]) * lax.axis_size(groups[1])
    blocks = cut_along(array, split_dim, length)
    return laid_out(moved_by_axis(blocks, groups, order), concat_dim)


def slot_table(expert_ids, experts_all, capacity):
    pairs = expert_ids.reshape(-1)
    count = pairs.shape[0]
    onehot = (pairs[:, None] == jnp.arange(experts_all, dtype=jnp.int32)[None, :]).astype(jnp.int32)
    before = jnp.cumsum(onehot, axis=0) - onehot
    position = jnp.sum(before * onehot, axis=1)
    dest = pairs * capacity + position
    filled = (
        jnp.zeros((experts_all * capacity,), jnp.int32)
        .at[dest]
        .set(jnp.arange(count, dtype=jnp.int32) + 1)
    )
    return (dest, filled)


def gather_rows(tokens, cotangent, combine, filled, top):
    live = filled > 0
    pair = jnp.maximum(filled - 1, 0)
    source = pair // top
    rows_x = jnp.where(live[:, None], jnp.take(tokens, source, axis=0), jnp.zeros((), tokens.dtype))
    rows_dy = jnp.where(
        live[:, None], jnp.take(cotangent, source, axis=0), jnp.zeros((), cotangent.dtype)
    )
    rows_c = jnp.where(
        live, jnp.take(combine.reshape(-1), pair, axis=0), jnp.zeros((), combine.dtype)
    )
    return (rows_x, rows_dy, rows_c)


def forward_part(rows_x, gate_mat, up_mat, down_mat):
    gate = jnp.dot(rows_x, gate_mat, preferred_element_type=jnp.float32)
    up = jnp.dot(rows_x, up_mat, preferred_element_type=jnp.float32)
    sig = jax.nn.sigmoid(gate)
    act = gate * sig
    hidden = (act * up).astype(jnp.bfloat16)
    output = jnp.dot(hidden, down_mat, preferred_element_type=jnp.float32)
    return (gate, up, sig, act, hidden, output)


def backward_part(state, rows_dy, rows_c, gate_mat, up_mat, down_mat):
    gate, up, sig, act, hidden, output = state
    comb_grad = jnp.sum(rows_dy.astype(jnp.float32) * output, axis=1)
    scaled = (rows_c[:, None] * rows_dy.astype(jnp.float32)).astype(jnp.bfloat16)
    last = (((1,), (1,)), ((), ()))
    hidden_grad = lax.dot_general(scaled, down_mat, last, preferred_element_type=jnp.float32)
    gate_d = (hidden_grad * up * (sig * (1.0 + gate * (1.0 - sig)))).astype(jnp.bfloat16)
    up_d = (hidden_grad * act).astype(jnp.bfloat16)
    row_grad = lax.dot_general(gate_d, gate_mat, last, preferred_element_type=jnp.float32)
    row_grad = (
        row_grad + lax.dot_general(up_d, up_mat, last, preferred_element_type=jnp.float32)
    ).astype(jnp.bfloat16)
    return (comb_grad, scaled, gate_d, up_d, row_grad)


def shards(tokens, cotangent, expert_ids, combine, w_gate, w_up, w_down):
    first = (((0,), (0,)), ((), ()))
    local_experts = w_gate.shape[0]
    groups = lax.axis_size(EXPERT)
    experts_all = local_experts * groups
    tok_rows, top = expert_ids.shape
    feature = tokens.shape[1]
    capacity = 2 * tok_rows * top // experts_all
    dest, filled = slot_table(expert_ids, experts_all, capacity)
    rows_x, rows_dy, rows_c = gather_rows(tokens, cotangent, combine, filled, top)
    rows_x = rows_x.reshape(experts_all, capacity, feature)
    rows_dy = rows_dy.reshape(experts_all, capacity, feature)
    rows_c = rows_c.reshape(experts_all, capacity)
    recv_x = lax.all_to_all(rows_x, EXPERT, split_axis=0, concat_axis=1, tiled=True)
    states = forward_part(recv_x[0], w_gate[0], w_up[0], w_down[0])
    recv_dy, recv_c = (
        lax.all_to_all(rows_dy, EXPERT, split_axis=0, concat_axis=1, tiled=True),
        lax.all_to_all(
            rows_c.astype(jnp.bfloat16), EXPERT, split_axis=0, concat_axis=1, tiled=True
        ).astype(rows_c.dtype),
    )
    comb_grad, scaled, gate_d, up_d, row_grad = backward_part(
        states, recv_dy[0], recv_c[0], w_gate[0], w_up[0], w_down[0]
    )
    row_list = [row_grad]
    comb_list = [comb_grad]
    inputs = recv_x[0]
    hidden = states[4]
    gate_terms = [lax.dot_general(inputs, gate_d, first, preferred_element_type=jnp.float32)]
    up_terms = [lax.dot_general(inputs, up_d, first, preferred_element_type=jnp.float32)]
    down_terms = [lax.dot_general(hidden, scaled, first, preferred_element_type=jnp.float32)]
    summed = tuple(
        (
            part.astype(jnp.float32)
            for part in one_scatter(
                (
                    jnp.stack(gate_terms).astype(jnp.bfloat16),
                    jnp.stack(up_terms).astype(jnp.bfloat16),
                    jnp.stack(down_terms).astype(jnp.bfloat16),
                ),
                "dp",
                (1, 1, 1),
            )
        )
    )
    gate_grad = summed[0].astype(jnp.bfloat16)
    up_grad = summed[1].astype(jnp.bfloat16)
    down_grad = summed[2].astype(jnp.bfloat16)
    back_rows, back_comb = (
        core_and_chips(jnp.stack(row_list), ("expert_0", "expert_1"), (1, 0), 1, 0),
        core_and_chips(
            jnp.stack(comb_list).astype(jnp.bfloat16), ("expert_0", "expert_1"), (1, 0), 1, 0
        ).astype(jnp.float32),
    )
    flat_rows = back_rows.reshape(experts_all * capacity, feature)
    picked = jnp.take(flat_rows, dest, axis=0).reshape(tok_rows, top, feature)
    input_grad = jnp.sum(picked.astype(jnp.float32), axis=1).astype(jnp.bfloat16)
    combine_grad = jnp.take(back_comb.reshape(-1), dest, axis=0).reshape(tok_rows, top)
    return (input_grad, combine_grad, gate_grad, up_grad, down_grad)


def solution(mesh):
    torus = Mesh(mesh.devices.reshape(mesh.shape["dp"], 2, 2), ("dp", "expert_0", "expert_1"))
    return jax.shard_map(
        shards,
        mesh=torus,
        in_specs=(
            P(DP_EXPERT, None),
            P(DP_EXPERT, None),
            P(DP_EXPERT, None),
            P(DP_EXPERT, None),
            P(EXPERT, None, None),
            P(EXPERT, None, None),
            P(EXPERT, None, None),
        ),
        out_specs=(
            P(DP_EXPERT, None),
            P(DP_EXPERT, None),
            P(EXPERT, "dp", None),
            P(EXPERT, "dp", None),
            P(EXPERT, "dp", None),
        ),
        check_vma=False,
    )
```

profile of v0, /device:TPU:0, one launch (start us, length us, event | category | flops | bytes accessed | tf_op | source)
XLA Modules:
  0.0 417.1 jit_solution(17223580062550271202)
XLA Ops:
  12.6 3.4 gather_fusion
  16.6 3.3 all-to-all-start
  19.9 6.4 %gather_fusion.3 = bf16[512,2048]{1,0:T(8,128)(2,1)} fusion(bf16[128,2048]{1,0:T(8,128)(2,1)} %param.10, s32[1024]{0:T(1024)S(1)} %pad_clamp_fusion.1), kind=kCustom, calls=%fused_computation.clone | custom fusion | bytes 4196352 | tf_op jit(solution)/shard_map/jit(_take)/gather | solution.py:71
  26.3 6.3 %gather_fusion.4 = bf16[512,2048]{1,0:T(8,128)(2,1)} fusion(bf16[128,2048]{1,0:T(8,128)(2,1)} %param.9, s32[1024]{0:T(1024)S(1)} %pad_clamp_fusion.1), kind=kCustom, calls=%fused_computation.1.clone | custom fusion | bytes 4196352 | tf_op jit(solution)/shard_map/jit(_take)/gather | solution.py:69
  32.6 4.0 select_select_fusion.1
  36.6 30.1 %all_to_all.48 = bf16[4,128,2048]{2,1,0:T(8,128)(2,1)} all-to-all(bf16[4,128,2048]{2,1,0:T(8,128)(2,1)} %bitcast.73), channel_id=1, replica_groups=mesh['dp'=32,'expert_0'=2,'expert_1'=2] {'expert_0','expert_1'}, dimensions={0} | all-to-all | bytes 4194304 | tf_op jit(solution)/shard_map/all_to_all | solution.py:117
  66.8 4.4 %all-to-all-start.1 = ((bf16[4,128,2048]{2,1,0:T(8,128)(2,1)}), bf16[4,128,2048]{2,1,0:T(8,128)(2,1)}, u32[]{:S(2)}, u32[]{:S(2)}) async-start(bf16[4,128,2048]{2,1,0:T(8,128)(2,1)} %bitcast.72), calls=%async_computation.1 | async-start | bytes 4194304 | tf_op jit(solution)/shard_map/all_to_all | solution.py:120
  71.5 5.5 %fusion.5 = f32[512,768]{1,0:T(8,128)} fusion(bf16[512,2048]{1,0:T(8,128)(2,1)} %bitcast.74, bf16[1,2048,768]{2,1,0:T(8,128)(2,1)} %param.13), kind=kOutput, calls=%fused_computation.19 | convolution fusion | flops 1610612736 | bytes 6815744 | tf_op jit(solution)/shard_map/dot_general | solution.py:80
  76.9 20.0 %all-to-all-done.1 = bf16[4,128,2048]{2,1,0:T(8,128)(2,1)} async-done(((bf16[4,128,2048]{2,1,0:T(8,128)(2,1)}), bf16[4,128,2048]{2,1,0:T(8,128)(2,1)}, u32[]{:S(2)}, u32[]{:S(2)}) %all-to-all-start.1) | async-done | bytes 2097184 | tf_op jit(solution)/shard_map/all_to_all | solution.py:120
  101.5 3.4 multiply_convert_fusion
  105.0 2.3 fusion.2
  107.3 3.5 convolution_convert_fusion
  110.8 4.8 %reshape_transpose_reshape.12 = bf16[32,49152]{1,0:T(8,128)(2,1)} reshape(bf16[768,2048]{1,0:T(8,128)(2,1)} %convolution_convert_fusion) | data formatting | bytes 6291456 | tf_op jit(solution)/shard_map/reshape;transpose;reshape | solution.py:19
  115.6 5.3 %convolution_convert_fusion.1 = bf16[2048,768]{1,0:T(8,128)(2,1)} fusion(bf16[512,2048]{1,0:T(8,128)(2,1)} %bitcast.75, bf16[512,768]{1,0:T(8,128)(2,1)} %get-tuple-element.29), kind=kOutput, calls=%fused_computation.15 | convolution fusion | flops 1612185600 | bytes 6029312 | tf_op jit(solution)/shard_map/dot_general | solution.py:133
  120.9 4.8 %reshape_transpose_reshape.11 = bf16[32,49152]{1,0:T(8,128)(2,1)} reshape(bf16[2048,768]{1,0:T(8,128)(2,1)} %convolution_convert_fusion.1) | data formatting | bytes 6291456 | tf_op jit(solution)/shard_map/reshape;transpose;reshape | solution.py:19
  125.7 5.3 %convolution_convert_fusion.2 = bf16[2048,768]{1,0:T(8,128)(2,1)} fusion(bf16[512,2048]{1,0:T(8,128)(2,1)} %bitcast.76, bf16[512,768]{1,0:T(8,128)(2,1)} %get-tuple-element.28), kind=kOutput, calls=%fused_computation.16 | convolution fusion | flops 1612185600 | bytes 6029312 | tf_op jit(solution)/shard_map/dot_general | solution.py:132
  131.0 4.9 %reshape_transpose_reshape.10 = bf16[32,49152]{1,0:T(8,128)(2,1)} reshape(bf16[2048,768]{1,0:T(8,128)(2,1)} %convolution_convert_fusion.2) | data formatting | bytes 6291456 | tf_op jit(solution)/shard_map/reshape;transpose;reshape | solution.py:19
  135.8 10.9 %pad_maximum_fusion = bf16[32,147456]{1,0:T(8,128)(2,1)} fusion(bf16[32,49152]{1,0:T(8,128)(2,1)} %reshape_transpose_reshape.12, bf16[32,49152]{1,0:T(8,128)(2,1)} %reshape_transpose_reshape.11, bf16[32,49152]{1,0:T(8,128)(2,1)} %reshape_transpose_reshape.10), kind=kLoop, calls=%fused_computation.6 | loop fusion | flops 28311552 | bytes 18874368 | tf_op jit(solution)/shard_map/concatenate | solution.py:19
  146.7 9.7 %reshape.195 = bf16[36864,128]{1,0:T(8,128)(2,1)} reshape(bf16[32,147456]{1,0:T(8,128)(2,1)} %pad_maximum_fusion) | data formatting | bytes 18874368 | tf_op jit(solution)/shard_map/reshape | solution.py:21
  156.5 4.0 fusion.3
  165.2 3.5 fusion.1
  168.7 3.7 all_to_all.49
  172.4 4.8 %all-to-all-start.3 = ((bf16[2,2,1,128,2048]{4,3,0,2,1:T(8,128)(2,1)}), bf16[2,2,1,128,2048]{4,3,0,2,1:T(8,128)(2,1)}, u32[]{:S(2)}, u32[]{:S(2)}) async-start(bf16[2,2,1,128,2048]{4,3,0,2,1:T(8,128)(2,1)} %copy.40), calls=%async_computation.3 | async-start | bytes 4194304 | tf_op jit(solution)/shard_map/all_to_all | solution.py:40
  177.8 2.4 all-to-all-done.3
  180.2 3.2 all-to-all-start.6
  183.4 3.2 copy.41
  187.1 5.1 %all-to-all-start.4 = ((bf16[2,2,1,128,2048]{4,3,1,2,0:T(8,128)(2,1)}), bf16[2,2,1,128,2048]{4,3,1,2,0:T(8,128)(2,1)}, u32[]{:S(2)}, u32[]{:S(2)}) async-start(bf16[2,2,1,128,2048]{4,3,1,2,0:T(8,128)(2,1)} %copy.41), calls=%async_computation.4 | async-start | bytes 4194304 | tf_op jit(solution)/shard_map/all_to_all | solution.py:40
  195.1 27.1 %all-to-all-done.4 = bf16[2,2,1,128,2048]{4,3,1,2,0:T(8,128)(2,1)} async-done(((bf16[2,2,1,128,2048]{4,3,1,2,0:T(8,128)(2,1)}), bf16[2,2,1,128,2048]{4,3,1,2,0:T(8,128)(2,1)}, u32[]{:S(2)}, u32[]{:S(2)}) %all-to-all-start.4) | async-done | bytes 2097184 | tf_op jit(solution)/shard_map/all_to_all | solution.py:40
  222.2 5.3 %gather_fusion.1 = bf16[256,2048]{1,0:T(8,128)(2,1)} fusion(bf16[512,2048]{1,0:T(8,128)(2,1)} %bitcast.14, s32[1024]{0:T(1024)S(1)} %pad_clamp_fusion), kind=kCustom, calls=%fused_computation.3 | custom fusion | bytes 2098176 | tf_op jit(solution)/shard_map/jit(_take)/gather | solution.py:159
  227.5 2.5 gather.21
  230.0 4.4 %fusion.17 = bf16[128,2048]{1,0:T(8,128)(2,1)} fusion(bf16[128,2,2048]{2,1,0:T(2,128)(2,1)} %gather.21, pred[128,2]{1,0:T(8,128)(4,1)S(1)} %get-tuple-element.22), kind=kLoop, calls=%fused_computation.36 | loop fusion | flops 786432 | bytes 1573120 | tf_op jit(solution)/shard_map/reduce_sum | solution.py:160
  234.4 172.7 %reduce-scatter.2.cloned.1.call-done = bf16[1152,128]{1,0:T(8,128)(2,1)} async-done(((bf16[36864,128]{1,0:T(8,128)(2,1)}), bf16[1152,128]{1,0:T(8,128)(2,1)}) %reduce-scatter.2.cloned.1.call-update) | async-done | bytes 294928 | tf_op jit(solution)/shard_map/reduce_scatter | solution.py:22
  (63 shorter events, 22.5 us)
Async XLA Ops:
  7.2 94.2 %copy-start = (bf16[1,2048,768]{2,1,0:T(8,128)(2,1)S(1)}, bf16[1,2048,768]{2,1,0:T(8,128)(2,1)}, u32[]{:S(2)}) copy-start(bf16[1,2048,768]{2,1,0:T(8,128)(2,1)} %param.14) | copy-start | bytes 9437188
  16.6 20.1 %all-to-all-start = ((bf16[4,1,128]{2,1,0:T(2,128)(2,1)}), bf16[4,1,128]{2,1,0:T(2,128)(2,1)S(1)}, u32[]{:S(2)}, u32[]{:S(2)}) async-start(bf16[4,1,128]{2,1,0:T(2,128)(2,1)} %copy.39), calls=%async_computation | async-start | bytes 4096 | tf_op jit(solution)/shard_map/all_to_all | solution.py:121
  66.8 30.2 %all-to-all-start.1 = ((bf16[4,128,2048]{2,1,0:T(8,128)(2,1)}), bf16[4,128,2048]{2,1,0:T(8,128)(2,1)}, u32[]{:S(2)}, u32[]{:S(2)}) async-start(bf16[4,128,2048]{2,1,0:T(8,128)(2,1)} %bitcast.72), calls=%async_computation.1 | async-start | bytes 4194304 | tf_op jit(solution)/shard_map/all_to_all | solution.py:120
  71.2 335.8 %reduce-scatter.2.cloned.1.call-start = ((), (), s32[]{:S(2)}) async-start(), calls=%async_computation.8 | async-start | bytes 9732096 | tf_op jit(solution)/shard_map/reduce_scatter | solution.py:22
  97.0 2.5 copy-start.2
  99.5 1.9 copy-start.1
  99.5 2.0 copy-start.7
  105.0 2.3 copy-start.5
  156.5 4.0 copy-start.4
  162.3 2.6 copy-start.3
  162.4 2.8 copy-start.6
  172.4 7.8 %all-to-all-start.3 = ((bf16[2,2,1,128,2048]{4,3,0,2,1:T(8,128)(2,1)}), bf16[2,2,1,128,2048]{4,3,0,2,1:T(8,128)(2,1)}, u32[]{:S(2)}, u32[]{:S(2)}) async-start(bf16[2,2,1,128,2048]{4,3,0,2,1:T(8,128)(2,1)} %copy.40), calls=%async_computation.3 | async-start | bytes 4194304 | tf_op jit(solution)/shard_map/all_to_all | solution.py:40
  180.2 6.9 %all-to-all-start.6 = ((bf16[2,2,1,128]{3,1,2,0:T(2,128)(2,1)}), bf16[2,2,1,128]{3,1,2,0:T(2,128)(2,1)S(1)}, u32[]{:S(2)}, u32[]{:S(2)}) async-start(bf16[2,2,1,128]{3,1,2,0:T(2,128)(2,1)} %copy.43), calls=%async_computation.6 | async-start | bytes 2048 | tf_op jit(solution)/shard_map/all_to_all | solution.py:40
  187.1 35.1 %all-to-all-start.4 = ((bf16[2,2,1,128,2048]{4,3,1,2,0:T(8,128)(2,1)}), bf16[2,2,1,128,2048]{4,3,1,2,0:T(8,128)(2,1)}, u32[]{:S(2)}, u32[]{:S(2)}) async-start(bf16[2,2,1,128,2048]{4,3,1,2,0:T(8,128)(2,1)} %copy.41), calls=%async_computation.4 | async-start | bytes 4194304 | tf_op jit(solution)/shard_map/all_to_all | solution.py:40
Sparse Core Ops, SparseCore 0:
  156.6 250.4 reduce-scatter.1
where the time goes:
time: 418 us; the launch traced here: 417 us
  waiting for transfers between devices  223 us (53%)
  local copies, waits for them, and re-layouts  65.9 us (16%)
  matrix products  34.2 us (8%)
  blocking collectives  33.8 us (8%)
  other arithmetic  25.2 us (6%)
  starting transfers between devices  21.1 us (5%)
  between operations  14.3 us (3%)
    reduce_scatter x1, waiting for transfers between devices, one_scatter(): lax.psum_scatter(lines, axis, tiled=True).reshape(-1)  173 us
    all_to_all x1, blocking collectives, shards(): lax.all_to_all(rows_x, EXPERT, split_axis=0, concat_axis=1, tiled=True)  30.1 us
    all_to_all x3, waiting for transfers between devices, moved_by_axis(): lax.all_to_all(blocks, axes[k], split_axis=k, concat_axis=k, tiled=True)  30 us
    all_to_all x1, waiting for transfers between devices, shards(): lax.all_to_all(rows_dy, EXPERT, split_axis=0, concat_axis=1, tiled=True)  20 us
    another operation x3, local copies, waits for them, and re-layouts, one_scatter(): lines = jnp.concatenate([b.reshape(length, -1) for b in blocks], axis=1)  14.5 us
    all_to_all x3, starting transfers between devices, moved_by_axis(): lax.all_to_all(blocks, axes[k], split_axis=k, concat_axis=k, tiled=True)  13.1 us
    concatenate x1, other arithmetic, one_scatter(): lines = jnp.concatenate([b.reshape(length, -1) for b in blocks], axis=1)  10.9 us
    reshape x1, local copies, waits for them, and re-layouts, one_scatter(): jnp.pad(lines, ((0, 0), (0, extent * 128 - lines.shape[1])))  9.71 us
  transfers between devices with their start and end apart: 6, of which 5 were waited for; matrix products, arithmetic and copies ran while one was open for 12% of the time, Pallas kernels for 0%

commit v1 on v0

v1 whole, which is shorter than its diff:
```python
import jax
import jax.numpy as jnp
from jax import lax
from jax.experimental import pallas as pl
from jax.experimental.pallas import tpu as pltpu
from jax.sharding import PartitionSpec as P

MESH = pl.DeviceIdType.MESH
BF16 = jnp.bfloat16
F32 = jnp.float32
D = 2048
FF = 768
T = 128
N_SEM = 160


def mod4(v):
    return lax.rem(v + 8, 4)


def nt(a, b):
    return lax.dot_general(a, b, (((1,), (1,)), ((), ())), preferred_element_type=F32)


def nn(a, b):
    return jnp.dot(a, b, preferred_element_type=F32)


class Wire:
    def __init__(self, send, recv):
        self.send, self.recv, self.count, self.all = send, recv, 0, []

    def make(self, src, dst, device):
        i = self.count
        self.count += 1
        copy = pltpu.make_async_remote_copy(
            src_ref=src,
            dst_ref=dst,
            send_sem=self.send.at[i],
            recv_sem=self.recv.at[i],
            device_id=device,
            device_id_type=MESH,
        )
        self.all.append(copy)
        copy.start()
        return copy


class Stream:
    def __init__(self, first, partial, recv1, gathered, recv2, recv3):
        self.first, self.partial, self.recv1 = first, partial, recv1
        self.gathered, self.recv2, self.recv3 = gathered, recv2, recv3
        self.flight = {}

    def chunk(self, way, c):
        return (c, way) if self.first == "x" else (slice(None), way, c)


def kernel(
    x_hbm,
    dy_hbm,
    ids_ref,
    comb_ref,
    wg_hbm,
    wu_hbm,
    wd_hbm,
    ig_ref,
    cg_ref,
    gg_ref,
    ug_ref,
    dg_ref,
    wg,
    wu,
    wd,
    x,
    dy,
    xt,
    act,
    dact,
    hid,
    hg,
    hc,
    hct,
    gd,
    ud,
    weight_rows,
    weight_cols,
    cg_part,
    cg_rows,
    cg_in,
    rg,
    rc,
    rz,
    pd,
    pg,
    rd1,
    rg1,
    qd,
    rd2,
    rg2,
    rd3,
    rg3,
    local_sem,
    send_sem,
    recv_sem,
):
    dp, ex = lax.axis_index("dp"), lax.axis_index("expert")
    ix, zh, iy = lax.div(dp, 8), lax.rem(lax.div(dp, 4), 2), lax.rem(dp, 4)
    zl, core = lax.div(ex, 2), lax.rem(ex, 2)

    def at(a, b, c):
        return {"dp": a * 8 + b * 4 + c, "expert": ex}

    x_next, x_prev = at(mod4(ix + 1), zh, iy), at(mod4(ix - 1), zh, iy)
    y_next, y_prev = at(ix, zh, mod4(iy + 1)), at(ix, zh, mod4(iy - 1))
    z_far = at(ix, 1 - zh, iy)
    mate = {"dp": dp, "expert": zl * 2 + 1 - core}
    z_near = {"dp": dp, "expert": (1 - zl) * 2 + core}
    z_diag = {"dp": dp, "expert": (1 - zl) * 2 + 1 - core}

    loads = [
        pltpu.make_async_copy(x_hbm, x.at[pl.ds(0, T)], local_sem.at[0]),
        pltpu.make_async_copy(dy_hbm, dy.at[pl.ds(0, T)], local_sem.at[1]),
        pltpu.make_async_copy(wg_hbm.at[0], wg, local_sem.at[2]),
        pltpu.make_async_copy(wu_hbm.at[0], wu, local_sem.at[3]),
        pltpu.make_async_copy(wd_hbm.at[0], wd, local_sem.at[4]),
    ]
    for load in loads:
        load.start()

    barrier = pltpu.get_barrier_semaphore()
    peers = (x_next, x_prev, y_next, y_prev, z_far, mate, z_near, z_diag)
    for peer in peers:
        pl.semaphore_signal(barrier, inc=1, device_id=peer, device_id_type=MESH)
    pl.semaphore_wait(barrier, len(peers))

    wire = Wire(send_sem, recv_sem)

    loads[0].wait()
    x_mate = wire.make(x.at[pl.ds(0, T)], x.at[pl.ds(T, T)], mate)
    x_near = [
        wire.make(x.at[pl.ds(64 * j, 64)], x.at[pl.ds(2 * T + 64 * j, 64)], z_near)
        for j in range(2)
    ]
    loads[1].wait()
    dy_mate = wire.make(dy.at[pl.ds(0, T)], dy.at[pl.ds(T, T)], mate)
    lane = lax.broadcasted_iota(jnp.int32, (T, T), 1)
    dense = jnp.zeros((T, T), F32)
    for k in range(2):
        dense += jnp.where(ids_ref[:, k : k + 1] == lane, comb_ref[:, k : k + 1], 0.0)
    weight_rows[0] = jnp.transpose(dense)[0:8]
    w_in = [
        wire.make(weight_rows.at[0], weight_rows.at[j], to)
        for j, to in ((1, mate), (2, z_near), (3, z_diag))
    ]
    dy_near = [
        wire.make(dy.at[pl.ds(32 * j, 32)], dy.at[pl.ds(2 * T + 32 * j, 32)], z_near)
        for j in range(4)
    ]

    def pass_on(arrivals, ref, rows):
        out = []
        for j, arrival in enumerate(arrivals):
            arrival.wait_recv()
            out.append(
                wire.make(
                    ref.at[pl.ds(2 * T + rows * j, rows)],
                    ref.at[pl.ds(3 * T + rows * j, rows)],
                    mate,
                )
            )
        return out

    def column_weights(slot):
        row = weight_rows[slot, pl.ds(ex, 1), :]
        weight_cols[slot * T : slot * T + T, :] = jnp.transpose(jnp.broadcast_to(row, (T, T)))

    def spread(start):
        col = weight_cols[pl.ds(start, 16), :]
        return jnp.concatenate([col] * 6, axis=1)

    def turned(r0):
        def body(j, carry):
            cols = pl.ds(pl.multiple_of(j * 256, 256), 256)
            xt[cols, r0 : r0 + 256] = jnp.transpose(x[r0 : r0 + 256, cols])
            return carry

        lax.fori_loop(0, D // 256, body, 0)

    def forward(r0):
        def matmul(n, carry):
            cols = pl.ds(pl.multiple_of(n * 256, 256), 256)
            act[:, cols] = nn(x[r0 : r0 + 256, :], wg[:, cols])
            dact[:, cols] = nn(x[r0 : r0 + 256, :], wu[:, cols])
            return carry

        lax.fori_loop(0, FF // 256, matmul, 0)

        def pointwise(i, carry):
            rows = pl.ds(pl.multiple_of(i * 16, 16), 16)
            gate, up = act[rows, :], dact[rows, :]
            s = jax.nn.sigmoid(gate)
            a = gate * s
            h = a * up
            act[rows, :] = a
            dact[rows, :] = up * s * (1.0 + gate * (1.0 - s))
            hid[rows, :] = h
            hc[rows, :] = (h * spread(pl.multiple_of(r0 + i * 16, 16))).astype(BF16)
            return carry

        lax.fori_loop(0, 16, pointwise, 0)

        def turn(n, carry):
            cols = pl.ds(pl.multiple_of(n * 256, 256), 256)
            hct[cols, r0 : r0 + 256] = jnp.transpose(hc[:, cols])
            return carry

        lax.fori_loop(0, FF // 256, turn, 0)

    def backward(r0):
        def matmul(n, carry):
            cols = pl.ds(pl.multiple_of(n * 256, 256), 256)
            hg[:, cols] = nt(dy[r0 : r0 + 256, :], wd[cols, :])
            return carry

        lax.fori_loop(0, FF // 256, matmul, 0)

        def pointwise(i, carry):
            rows = pl.ds(pl.multiple_of(i * 16, 16), 16)
            full = pl.ds(pl.multiple_of(r0 + i * 16, 16), 16)
            g = hg[rows, :]
            prod = g * hid[rows, :]
            total = prod[:, 0:128]
            for j in range(1, 6):
                total += prod[:, 128 * j : 128 * j + 128]
            cg_part[full, :] = total
            g = g * spread(pl.multiple_of(r0 + i * 16, 16))
            gd[full, :] = (g * dact[rows, :]).astype(BF16)
            ud[full, :] = (g * act[rows, :]).astype(BF16)
            return carry

        lax.fori_loop(0, 16, pointwise, 0)

    loads[2].wait()
    loads[3].wait()
    x_mate.wait_recv()
    for copy in w_in:
        copy.wait_recv()
    for slot in range(4):
        column_weights(slot)
    forward(0)
    x_diag = pass_on(x_near[0:1], x, 64)
    turned(0)
    loads[4].wait()
    dy_mate.wait_recv()
    backward(0)
    x_near[1].wait_recv()
    x_diag.append(
        wire.make(x.at[pl.ds(2 * T + 64, 64)], x.at[pl.ds(3 * T + 64, 64)], mate)
    )

    for copy in x_diag:
        copy.wait_recv()
    forward(256)
    turned(256)
    dy_diag = pass_on(dy_near, dy, 32)
    for copy in dy_diag:
        copy.wait_recv()

    def stream(first, partial, recv1, gathered, recv2, recv3):
        return Stream(first, partial, recv1, gathered, recv2, recv3)

    d0 = stream("x", pd.at[0], rd1.at[0], qd.at[0], rd2.at[0], rd3.at[0])
    d1 = stream("x", pd.at[1], rd1.at[1], qd.at[1], rd2.at[1], rd3.at[1])
    g0 = stream("x", pg.at[0], rg1.at[0], None, rg2.at[0], rg3.at[0])
    g1 = stream("y", pg.at[1], rg1.at[1], None, rg2.at[1], rg3.at[1])
    u0 = stream("y", pg.at[2], rg1.at[2], None, rg2.at[2], rg3.at[2])
    u1 = stream("y", pg.at[3], rg1.at[3], None, rg2.at[3], rg3.at[3])

    def down_part(dst, c0):
        def body(n, carry):
            src = pl.ds(pl.multiple_of(c0 + n * 256, 256), 256)
            cols = pl.ds(pl.multiple_of(n * 256, 256), 256)
            r = nn(hct[...], dy[:, src]).astype(BF16)
            dst[:, :, :, cols] = r.reshape(4, 2, 96, 256)
            return carry

        lax.fori_loop(0, 4, body, 0)

    def up_part(dst, right, c0):
        def body(m, carry):
            rows = pl.ds(pl.multiple_of(m * 256, 256), 256)
            r = nn(xt[rows, :], right[:, c0 : c0 + 384]).astype(BF16)
            dst[lax.div(m, 2), lax.rem(m, 2)] = r.reshape(4, 64, 384)
            return carry

        lax.fori_loop(0, 8, body, 0)

    def ring1(st, way):
        i = ix if st.first == "x" else iy
        sign = 1 - 2 * way
        near = ((x_next, x_prev) if st.first == "x" else (y_next, y_prev))[way]
        return i, sign, near

    def ring2(st, way):
        i = iy if st.first == "x" else ix
        sign = 1 - 2 * way
        near = ((y_next, y_prev) if st.first == "x" else (x_next, x_prev))[way]
        return i, sign, near

    def launch(st):
        for way in range(2):
            i, sign, near = ring1(st, way)
            c = mod4(i - sign)
            src = st.partial.at[st.chunk(way, c)]
            st.flight[way] = wire.make(src, st.recv1.at[way, 0], near)

    def settled(st, way, c):
        return st.gathered.at[way, c] if st.gathered is not None else st.recv1.at[way, 2, c]

    def step1(st, s):
        for way in range(2):
            i, sign, near = ring1(st, way)
            c = mod4(i - (2 + s) * sign)
            st.flight[way].wait_recv()
            if st.gathered is None:
                for j in range(4):
                    own = st.partial[c, way, j] if st.first == "x" else st.partial[j, way, c]
                    total = st.recv1[way, s, j].astype(F32) + own.astype(F32)
                    st.recv1[way, s, j] = total.astype(BF16)
            elif s < 2:
                for j in range(4):
                    cols = slice(256 * j, 256 * j + 256)
                    total = st.recv1[way, s, :, cols].astype(F32)
                    total += st.partial[c, way, :, cols].astype(F32)
                    st.recv1[way, s, :, cols] = total.astype(BF16)
            else:
                for j in range(2):
                    lo = slice(256 * j, 256 * j + 256)
                    hi = slice(512 + 256 * j, 768 + 256 * j)
                    left = st.recv1[way, s, :, lo].astype(F32)
                    left += st.partial[c, way, :, lo].astype(F32)
                    right = st.recv1[way, s, :, hi].astype(F32)
                    right += st.partial[c, way, :, hi].astype(F32)
                    for q in range(4):
                        both = jnp.concatenate(
                            [left[24 * q : 24 * q + 24], right[24 * q : 24 * q + 24]], axis=0
                        )
                        st.gathered[way, q, :, lo] = both.astype(BF16)
            if s < 2:
                st.flight[way] = wire.make(st.recv1.at[way, s], st.recv1.at[way, s + 1], near)
            else:
                i, sign, near = ring2(st, way)
                src = settled(st, way, mod4(i - sign))
                st.flight[way] = wire.make(src, st.recv2.at[way, 0], near)

    def step2(st, s):
        for way in range(2):
            i, sign, near = ring2(st, way)
            c = mod4(i - (2 + s) * sign)
            st.flight[way].wait_recv()
            total = st.recv2[way, s].astype(F32) + settled(st, way, c)[...].astype(F32)
            st.recv2[way, s] = total.astype(BF16)
            if s < 2:
                st.flight[way] = wire.make(st.recv2.at[way, s], st.recv2.at[way, s + 1], near)
        if s == 2:
            st.flight[2] = wire.make(st.recv2.at[1 - zh, 2], st.recv3, z_far)

    def result(st):
        st.flight[2].wait_recv()
        return st.recv2[zh, 2].astype(F32) + st.recv3[...].astype(F32)

    down_part(d0.partial, 0)
    launch(d0)
    backward(256)
    up_part(g1.partial, gd, 384)
    launch(g1)
    down_part(d1.partial, 1024)
    launch(d1)
    up_part(u0.partial, ud, 0)
    launch(u0)
    up_part(g0.partial, gd, 0)
    launch(g0)
    up_part(u1.partial, ud, 384)
    launch(u1)

    def row_part(r0):
        def body(n, carry):
            cols = pl.ds(pl.multiple_of(n * 256, 256), 256)
            r = nt(gd[r0 : r0 + 256, :], wg[cols, :]) + nt(ud[r0 : r0 + 256, :], wu[cols, :])
            rg[r0 : r0 + 256, cols] = r.astype(BF16)
            return carry

        lax.fori_loop(0, D // 256, body, 0)

    order = (d0, g1, d1, u0, g0, u1)
    for st in order[0:2]:
        step1(st, 0)
    row_part(256)
    rc_far = wire.make(rg.at[pl.ds(3 * T, T)], rc.at[1], mate)
    for slot in range(4):
        row = jnp.sum(jnp.transpose(cg_part[slot * T : slot * T + T, :]), axis=0, keepdims=True)
        cg_rows[slot] = jnp.broadcast_to(row, (8, T))
    cg_copies = [
        wire.make(cg_rows.at[j], cg_in.at[j], to)
        for j, to in ((1, mate), (2, z_near), (3, z_diag))
    ]
    for st in order[2:4]:
        step1(st, 0)
    row_part(0)
    rc_near = wire.make(rg.at[pl.ds(T, T)], rc.at[0], mate)
    for st in order[4:6]:
        step1(st, 0)
    rc_far.wait_recv()

    def add_far(i, carry):
        rows = pl.ds(pl.multiple_of(i * 16, 16), 16)
        full = pl.ds(pl.multiple_of(2 * T + i * 16, 16), 16)
        total = rg[full, :].astype(F32) + rc[1, rows, :].astype(F32)
        rg[full, :] = total.astype(BF16)
        return carry

    lax.fori_loop(0, T // 16, add_far, 0)
    rz_in = wire.make(rg.at[pl.ds(2 * T, T)], rz, z_near)

    for st in order:
        step1(st, 1)

    ids = ids_ref[...]
    for copy in cg_copies:
        copy.wait_recv()
    answer = jnp.zeros((T, 2), F32)
    for j in range(4):
        row = cg_rows[0, 0:1, :] if j == 0 else cg_in[j, 0:1, :]
        cols = jnp.transpose(jnp.broadcast_to(row, (T, T)))[:, 0:2]
        answer += jnp.where(ids == jnp.bitwise_xor(ex, j), cols, 0.0)
    cg_ref[...] = answer

    for st in order:
        step1(st, 2)

    rc_near.wait_recv()
    rz_in.wait_recv()

    def add_rows(i, carry):
        rows = pl.ds(pl.multiple_of(i * 16, 16), 16)
        total = rg[rows, :].astype(F32) + rc[0, rows, :].astype(F32) + rz[rows, :].astype(F32)
        ig_ref[rows, :] = total.astype(BF16)
        return carry

    lax.fori_loop(0, T // 16, add_rows, 0)

    for s in range(3):
        for st in order:
            step2(st, s)
    for st, base in ((d0, 0), (d1, 1024)):
        r = result(st)
        dg_ref[0, :, base : base + 512] = r[0:24].astype(BF16)
        dg_ref[0, :, base + 512 : base + 1024] = r[24:48].astype(BF16)
    gg_ref[0, :, 384:768] = result(g1).astype(BF16)
    ug_ref[0, :, 0:384] = result(u0).astype(BF16)
    gg_ref[0, :, 0:384] = result(g0).astype(BF16)
    ug_ref[0, :, 384:768] = result(u1).astype(BF16)

    for copy in wire.all:
        copy.wait_send()


def shards(tokens, cotangent, expert_ids, combine, w_gate, w_up, w_down):
    hbm = pl.BlockSpec(memory_space=pl.ANY)
    vmem = pl.BlockSpec(memory_space=pltpu.VMEM)
    return pl.pallas_call(
        kernel,
        out_shape=(
            jax.ShapeDtypeStruct((T, D), BF16),
            jax.ShapeDtypeStruct((T, 2), F32),
            jax.ShapeDtypeStruct((1, 64, FF), BF16),
            jax.ShapeDtypeStruct((1, 64, FF), BF16),
            jax.ShapeDtypeStruct((1, 24, D), BF16),
        ),
        in_specs=[hbm, hbm, vmem, vmem, hbm, hbm, hbm],
        out_specs=(vmem, vmem, vmem, vmem, vmem),
        scratch_shapes=[
            pltpu.VMEM((D, FF), BF16),
            pltpu.VMEM((D, FF), BF16),
            pltpu.VMEM((FF, D), BF16),
            pltpu.VMEM((4 * T, D), BF16),
            pltpu.VMEM((4 * T, D), BF16),
            pltpu.VMEM((D, 4 * T), BF16),
            pltpu.VMEM((256, FF), F32),
            pltpu.VMEM((256, FF), F32),
            pltpu.VMEM((256, FF), F32),
            pltpu.VMEM((256, FF), F32),
            pltpu.VMEM((256, FF), BF16),
            pltpu.VMEM((FF, 4 * T), BF16),
            pltpu.VMEM((4 * T, FF), BF16),
            pltpu.VMEM((4 * T, FF), BF16),
            pltpu.VMEM((4, 8, T), F32),
            pltpu.VMEM((4 * T, T), F32),
            pltpu.VMEM((4 * T, T), F32),
            pltpu.VMEM((4, 8, T), F32),
            pltpu.VMEM((4, 8, T), F32),
            pltpu.VMEM((4 * T, D), BF16),
            pltpu.VMEM((2, T, D), BF16),
            pltpu.VMEM((T, D), BF16),
            pltpu.VMEM((2, 4, 2, 96, 1024), BF16),
            pltpu.VMEM((4, 4, 2, 4, 64, 384), BF16),
            pltpu.VMEM((2, 2, 3, 96, 1024), BF16),
            pltpu.VMEM((4, 2, 3, 4, 64, 384), BF16),
            pltpu.VMEM((2, 2, 4, 48, 512), BF16),
            pltpu.VMEM((2, 2, 3, 48, 512), BF16),
            pltpu.VMEM((4, 2, 3, 64, 384), BF16),
            pltpu.VMEM((2, 48, 512), BF16),
            pltpu.VMEM((4, 64, 384), BF16),
            pltpu.SemaphoreType.DMA((5,)),
            pltpu.SemaphoreType.DMA((N_SEM,)),
            pltpu.SemaphoreType.DMA((N_SEM,)),
        ],
        compiler_params=pltpu.CompilerParams(
            collective_id=0, has_side_effects=True, vmem_limit_bytes=62 * 1024 * 1024
        ),
        name="experts",
    )(tokens, cotangent, expert_ids, combine, w_gate, w_up, w_down)


def solution(mesh):
    both = ("dp", "expert")
    return jax.shard_map(
        shards,
        mesh=mesh,
        in_specs=(
            P(both, None),
            P(both, None),
            P(both, None),
            P(both, None),
            P("expert", None, None),
            P("expert", None, None),
            P("expert", None, None),
        ),
        out_specs=(
            P(both, None),
            P(both, None),
            P("expert", "dp", None),
            P("expert", "dp", None),
            P("expert", "dp", None),
        ),
        check_vma=False,
    )
```

time: 418 us -> 111 us (0.27)
  waiting for transfers between devices: 223 us -> 0 us
  Pallas kernels: 0 us -> 99.5 us
  local copies, waits for them, and re-layouts: 65.9 us -> 10.8 us
  matrix products: 34.2 us -> 0 us
  blocking collectives: 33.8 us -> 0 us
  other arithmetic: 25.2 us -> 0 us
  starting transfers between devices: 21.1 us -> 0 us
  between operations: 14.3 us -> 0.64 us
    reduce_scatter x1 -> x0, waiting for transfers between devices: 173 us -> none  [one_scatter(): lax.psum_scatter(lines, axis, tiled=True).reshape(-1)]
    pallas_call x0 -> x1, Pallas kernels: none -> 99.5 us  [shards(): pl.pallas_call(kernel, out_shape=(jax.ShapeDtypeStruct((T, D), BF16), jax...]
    all_to_all x5 -> x0, waiting for transfers between devices: 50 us -> none  [the longest x3 30 us: moved_by_axis(): lax.all_to_all(blocks, axes[k], split_axis=k, concat_axis=k, tiled=True)]
    dot_general x9 -> x0, matrix products: 34.2 us -> none  [the longest x1 5.45 us: forward_part(): gate = jnp.dot(rows_x, gate_mat, preferred_element_type=jnp.float32)]
    all_to_all x2 -> x0, blocking collectives: 33.8 us -> none  [the longest x1 30.1 us: shards(): lax.all_to_all(rows_x, EXPERT, split_axis=0, concat_axis=1, tiled=True)]
    gather x7 -> x0, local copies, waits for them, and re-layouts: 26 us -> none  [the longest x2 7.8 us: shards(): picked = jnp.take(flat_rows, dest, axis=0).reshape(tok_rows, top, feature)]
    all_to_all x5 -> x0, starting transfers between devices: 20.8 us -> none  [the longest x3 13.1 us: moved_by_axis(): lax.all_to_all(blocks, axes[k], split_axis=k, concat_axis=k, tiled=True)]
    another operation x6 -> x0, local copies, waits for them, and re-layouts: 16.2 us -> none  [the longest x3 14.5 us: one_scatter(): lines = jnp.concatenate([b.reshape(length, -1) for b in blocks], axis=1)]
  transfers between devices with their start and end apart: 6 -> 0, of which waited for: 5 -> 0; matrix products, arithmetic and copies ran while one was open for 12% -> 0% of each run, Pallas kernels for 0% -> 0%
where the time goes in v1:
time: 111 us
  Pallas kernels  99.5 us (90%)
  local copies, waits for them, and re-layouts  10.8 us (10%)
    pallas_call x1, Pallas kernels, shards(): pl.pallas_call(kernel, out_shape=(jax.ShapeDtypeStruct((T, D), BF16), jax...  99.5 us
    unnamed x6, local copies, waits for them, and re-layouts  9.32 us

profile of v1, /device:TPU:0, one launch (start us, length us, event | category | flops | bytes accessed | tf_op | source)
XLA Modules:
  0.0 111.0 jit_solution(9498147859311158341)
XLA Ops:
  0.6 1.4 %copy.12.ids_ref = s32[128,2]{1,0:T(8,128)} copy(s32[128,2]{0,1:T(2,128)} %param.9) | data formatting | bytes 2048 | tf_op args[2]
  2.0 1.4 %copy.13.comb_ref = f32[128,2]{1,0:T(8,128)} copy(f32[128,2]{0,1:T(2,128)} %param.10) | data formatting | bytes 2048 | tf_op args[3]
  3.5 99.5 %experts.1 = (bf16[128,2048]{1,0:T(8,128)(2,1)}, f32[128,2]{1,0:T(8,128)}, bf16[1,64,768]{2,1,0:T(8,128)(2,1)}, bf16[1,64,768]{2,1,0:T(8,128)(2,1)}, bf16[1,24,2048]{2,1,0:T(8,128)(2,1)}) custom-call(bf16[128,2048]{1,0:T(8,128)(2,1)} %x_hbm.1, bf16[128,2048]{1,0:T(8,128)(2,1)} %dy_hbm.1, s32[128,2]{1,0:T(8,128)} %copy.12.ids_ref, f32[128,2]{1,0:T(8,128)} %copy.13.comb_ref, ...), custom_call_target="tpu_custom_call" | custom-call | tf_op jit(solution)/shard_map/experts/pallas_call | solution.py:472
  103.0 1.5 %copy.14 = f32[128,2]{0,1:T(2,128)} copy(f32[128,2]{1,0:T(8,128)} %get-tuple-element.6) | data formatting | bytes 2048 | tf_op jit(solution)/shard_map/experts/pallas_call | solution.py:472
  104.5 1.9 %copy.19 = bf16[128,2048]{1,0:T(8,128)(2,1)} copy(bf16[128,2048]{1,0:T(8,128)(2,1)} %get-tuple-element.15) | data formatting | bytes 1048576
  106.3 1.5 %copy.20 = bf16[1,64,768]{2,1,0:T(8,128)(2,1)} copy(bf16[1,64,768]{2,1,0:T(8,128)(2,1)} %get-tuple-element.17) | data formatting | bytes 196608
  107.9 1.5 %copy.21 = bf16[1,64,768]{2,1,0:T(8,128)(2,1)} copy(bf16[1,64,768]{2,1,0:T(8,128)(2,1)} %get-tuple-element.18) | data formatting | bytes 196608
  109.4 1.5 %copy.22 = bf16[1,24,2048]{2,1,0:T(8,128)(2,1)} copy(bf16[1,24,2048]{2,1,0:T(8,128)(2,1)} %get-tuple-element.19) | data formatting | bytes 196608

commit v2 on v1

v2 whole, which is shorter than its diff:
```python
import jax
import jax.numpy as jnp
from jax import lax
from jax.experimental import pallas as pl
from jax.experimental.pallas import tpu as pltpu
from jax.sharding import PartitionSpec as P

MESH = pl.DeviceIdType.MESH
BF16 = jnp.bfloat16
F32 = jnp.float32
D = 2048
FF = 768
T = 128
N_SEM = 140


def mod4(v):
    return lax.rem(v + 8, 4)


def nt(a, b):
    return lax.dot_general(a, b, (((1,), (1,)), ((), ())), preferred_element_type=F32)


def nn(a, b):
    return jnp.dot(a, b, preferred_element_type=F32)


class Wire:
    def __init__(self, sems, other):
        self.sems, self.other, self.count, self.groups = sems, other, 0, []

    def sem(self):
        self.count += 1
        return self.sems.at[self.count - 1]

    def describe(self, src, dst, send, recv, device):
        return pltpu.make_async_remote_copy(
            src_ref=src,
            dst_ref=dst,
            send_sem=send,
            recv_sem=recv,
            device_id=device,
            device_id_type=MESH,
        )

    def group(self, total):
        send = self.sem()
        self.groups.append((send, total))
        return send

    def put(self, src, dst, device, send, recv):
        self.describe(src, dst, send, recv, device).start()

    def arrived(self, ref, recv):
        self.describe(ref, ref, recv, recv, self.other).wait_recv()

    def finish(self):
        for send, total in self.groups:
            self.describe(total, total, send, send, self.other).wait_send()


class Stream:
    def __init__(self, wire, first, partial, recv1, recv2, recv3):
        self.first, self.partial = first, partial
        self.recv1, self.recv2, self.recv3 = recv1, recv2, recv3
        self.send1, self.send2 = wire.group(recv1), wire.group(recv2)
        self.send3 = wire.group(recv3)
        self.sem1 = [wire.sem() for _ in range(3)]
        self.sem2 = [wire.sem() for _ in range(3)]
        self.sem3 = wire.sem()

    def chunk(self, way, c):
        return (c, way) if self.first == "x" else (slice(None), way, c)


def kernel(
    x_hbm,
    dy_hbm,
    ids_ref,
    comb_ref,
    wg_hbm,
    wu_hbm,
    wd_hbm,
    ig_hbm,
    cg_hbm,
    gg_hbm,
    ug_hbm,
    dg_hbm,
    wg,
    wu,
    wd,
    x,
    dy,
    xt,
    act,
    dact,
    hid,
    hg,
    hc,
    hct,
    gd,
    ud,
    weight_rows,
    weight_cols,
    cg_part,
    cg_rows,
    cg_in,
    rg,
    rc,
    rz,
    pd,
    pg,
    rd1,
    rg1,
    rd2,
    rg2,
    rd3,
    rg3,
    ig_out,
    cg_out,
    gg_out,
    ug_out,
    dg_out,
    local_sem,
    remote_sem,
):
    dp, ex = lax.axis_index("dp"), lax.axis_index("expert")
    ix, zh, iy = lax.div(dp, 8), lax.rem(lax.div(dp, 4), 2), lax.rem(dp, 4)
    zl, core = lax.div(ex, 2), lax.rem(ex, 2)

    def at(a, b, c):
        return {"dp": a * 8 + b * 4 + c, "expert": ex}

    x_next, x_prev = at(mod4(ix + 1), zh, iy), at(mod4(ix - 1), zh, iy)
    y_next, y_prev = at(ix, zh, mod4(iy + 1)), at(ix, zh, mod4(iy - 1))
    z_far = at(ix, 1 - zh, iy)
    mate = {"dp": dp, "expert": zl * 2 + 1 - core}
    z_near = {"dp": dp, "expert": (1 - zl) * 2 + core}
    z_diag = {"dp": dp, "expert": (1 - zl) * 2 + 1 - core}

    loads = [
        pltpu.make_async_copy(x_hbm, x.at[pl.ds(0, T)], local_sem.at[0]),
        pltpu.make_async_copy(dy_hbm, dy.at[pl.ds(0, T)], local_sem.at[1]),
        pltpu.make_async_copy(wg_hbm.at[0], wg, local_sem.at[2]),
        pltpu.make_async_copy(wu_hbm.at[0], wu, local_sem.at[3]),
        pltpu.make_async_copy(wd_hbm.at[0], wd, local_sem.at[4]),
    ]
    for load in loads:
        load.start()

    barrier = pltpu.get_barrier_semaphore()
    peers = (x_next, x_prev, y_next, y_prev, z_far, mate, z_near, z_diag)
    for peer in peers:
        pl.semaphore_signal(barrier, inc=1, device_id=peer, device_id_type=MESH)
    pl.semaphore_wait(barrier, len(peers))

    wire = Wire(remote_sem, mate)

    def slot_rows(ref, slot):
        return ref.at[pl.ds(slot * T, T)]

    def x_block(slot, j):
        return x.at[pl.ds(slot * T + 64 * j, 64)]

    def dy_block(slot, j):
        return dy.at[pl.ds(slot * T, T), pl.ds(512 * j, 512)]

    x_near_send, x_near = wire.group(slot_rows(x, 0)), [wire.sem() for _ in range(2)]
    x_mate_send, x_mate = wire.group(slot_rows(x, 0)), wire.sem()
    x_pass_send, x_diag = wire.group(slot_rows(x, 2)), [wire.sem() for _ in range(2)]
    dy_near_send, dy_near = wire.group(slot_rows(dy, 0)), [wire.sem() for _ in range(4)]
    dy_mate_send, dy_mate = wire.group(slot_rows(dy, 0)), wire.sem()
    dy_pass_send, dy_diag = wire.group(slot_rows(dy, 2)), [wire.sem() for _ in range(4)]
    w_send, w_in = wire.group(weight_rows.at[pl.ds(1, 3)]), wire.sem()

    expert = lax.broadcasted_iota(jnp.int32, (8, T), 0)
    dense = jnp.zeros((8, T), F32)
    for k in range(2):
        dense += jnp.where(ids_ref[k : k + 1, :] == expert, comb_ref[k : k + 1, :], 0.0)
    weight_rows[0] = dense
    for j, to in ((1, mate), (2, z_near), (3, z_diag)):
        wire.put(weight_rows.at[0], weight_rows.at[j], to, w_send, w_in)

    loads[0].wait()
    for j in range(2):
        wire.put(x_block(0, j), x_block(2, j), z_near, x_near_send, x_near[j])
    wire.put(slot_rows(x, 0), slot_rows(x, 1), mate, x_mate_send, x_mate)
    loads[1].wait()
    for j in range(4):
        wire.put(dy_block(0, j), dy_block(2, j), z_near, dy_near_send, dy_near[j])
    wire.put(slot_rows(dy, 0), slot_rows(dy, 1), mate, dy_mate_send, dy_mate)

    def pass_x(j):
        wire.arrived(x_block(2, j), x_near[j])
        wire.put(x_block(2, j), x_block(3, j), mate, x_pass_send, x_diag[j])

    def pass_dy(j):
        wire.arrived(dy_block(2, j), dy_near[j])
        wire.put(dy_block(2, j), dy_block(3, j), mate, dy_pass_send, dy_diag[j])

    def column_weights(slot):
        row = weight_rows[slot, pl.ds(ex, 1), :]
        weight_cols[slot * T : slot * T + T, :] = jnp.transpose(jnp.broadcast_to(row, (T, T)))

    def spread(start):
        col = weight_cols[pl.ds(start, 16), :]
        return jnp.concatenate([col] * 6, axis=1)

    def turned(r0):
        def body(j, carry):
            cols = pl.ds(pl.multiple_of(j * 256, 256), 256)
            xt[cols, r0 : r0 + 256] = jnp.transpose(x[r0 : r0 + 256, cols])
            return carry

        lax.fori_loop(0, D // 256, body, 0)

    def forward(r0):
        def matmul(n, carry):
            cols = pl.ds(pl.multiple_of(n * 256, 256), 256)
            act[:, cols] = nn(x[r0 : r0 + 256, :], wg[:, cols])
            dact[:, cols] = nn(x[r0 : r0 + 256, :], wu[:, cols])
            return carry

        lax.fori_loop(0, FF // 256, matmul, 0)

        def pointwise(i, carry):
            rows = pl.ds(pl.multiple_of(i * 16, 16), 16)
            gate, up = act[rows, :], dact[rows, :]
            s = jax.nn.sigmoid(gate)
            a = gate * s
            h = a * up
            act[rows, :] = a
            dact[rows, :] = up * s * (1.0 + gate * (1.0 - s))
            hid[rows, :] = h
            hc[rows, :] = (h * spread(pl.multiple_of(r0 + i * 16, 16))).astype(BF16)
            return carry

        lax.fori_loop(0, 16, pointwise, 0)

        def turn(n, carry):
            cols = pl.ds(pl.multiple_of(n * 256, 256), 256)
            hct[cols, r0 : r0 + 256] = jnp.transpose(hc[:, cols])
            return carry

        lax.fori_loop(0, FF // 256, turn, 0)

    def hidden_part(r0, first, j0, width):
        def matmul(n, carry):
            cols = pl.ds(pl.multiple_of(n * 256, 256), 256)
            r = nt(dy[r0 : r0 + 256, j0 : j0 + width], wd[cols, j0 : j0 + width])
            hg[:, cols] = r if first else hg[:, cols] + r
            return carry

        lax.fori_loop(0, FF // 256, matmul, 0)

    def backward(r0):
        def pointwise(i, carry):
            rows = pl.ds(pl.multiple_of(i * 16, 16), 16)
            full = pl.ds(pl.multiple_of(r0 + i * 16, 16), 16)
            g = hg[rows, :]
            prod = g * hid[rows, :]
            total = prod[:, 0:128]
            for j in range(1, 6):
                total += prod[:, 128 * j : 128 * j + 128]
            cg_part[full, :] = total
            g = g * spread(pl.multiple_of(r0 + i * 16, 16))
            gd[full, :] = (g * dact[rows, :]).astype(BF16)
            ud[full, :] = (g * act[rows, :]).astype(BF16)
            return carry

        lax.fori_loop(0, 16, pointwise, 0)

    loads[2].wait()
    loads[3].wait()
    wire.arrived(slot_rows(x, 1), x_mate)
    wire.arrived(weight_rows.at[pl.ds(1, 3)], w_in)
    for slot in range(4):
        column_weights(slot)
    forward(0)
    pass_x(0)
    turned(0)
    loads[4].wait()
    wire.arrived(slot_rows(dy, 1), dy_mate)
    hidden_part(0, True, 0, D)
    backward(0)
    pass_x(1)

    for j in range(2):
        wire.arrived(x_block(3, j), x_diag[j])
    forward(256)

    def down_stream(first, j):
        return Stream(wire, first, pd.at[j], rd1.at[j], rd2.at[j], rd3.at[j])

    def up_stream(first, j):
        return Stream(wire, first, pg.at[j], rg1.at[j], rg2.at[j], rg3.at[j])

    d = [down_stream(first, j) for j, first in enumerate("xyxy")]
    g0, g1, u0, u1 = [up_stream(first, j) for j, first in enumerate("xyxy")]

    def down_part(dst, c0):
        def body(n, carry):
            src = pl.ds(pl.multiple_of(c0 + n * 256, 256), 256)
            cols = pl.ds(pl.multiple_of(n * 256, 256), 256)
            r = nn(hct[...], dy[:, src]).reshape(4, 2, 4, 24, 256)
            dst[:, :, :, :, cols] = r.astype(BF16)
            return carry

        lax.fori_loop(0, 2, body, 0)

    def up_part(dst, right, c0):
        def body(m, carry):
            rows = pl.ds(pl.multiple_of(m * 256, 256), 256)
            r = nn(xt[rows, :], right[:, c0 : c0 + 384]).astype(BF16)
            dst[lax.div(m, 2), lax.rem(m, 2)] = r.reshape(4, 64, 384)
            return carry

        lax.fori_loop(0, 8, body, 0)

    def ring(first, way):
        i = ix if first == "x" else iy
        near = ((x_next, x_prev) if first == "x" else (y_next, y_prev))[way]
        return i, 1 - 2 * way, near

    def launch(st):
        for way in range(2):
            i, sign, near = ring(st.first, way)
            src = st.partial.at[st.chunk(way, mod4(i - sign))]
            wire.put(src, st.recv1.at[way, 0], near, st.send1, st.sem1[0])

    def step1(st, s):
        wire.arrived(st.recv1.at[:, s], st.sem1[s])
        for way in range(2):
            i, sign, near = ring(st.first, way)
            c = mod4(i - (2 + s) * sign)
            for j in range(4):
                own = st.partial[c, way, j] if st.first == "x" else st.partial[j, way, c]
                total = st.recv1[way, s, j].astype(F32) + own.astype(F32)
                st.recv1[way, s, j] = total.astype(BF16)
            if s < 2:
                wire.put(
                    st.recv1.at[way, s], st.recv1.at[way, s + 1], near, st.send1, st.sem1[s + 1]
                )
            else:
                i, sign, near = ring("y" if st.first == "x" else "x", way)
                src = st.recv1.at[way, 2, mod4(i - sign)]
                wire.put(src, st.recv2.at[way, 0], near, st.send2, st.sem2[0])

    def step2(st, s):
        wire.arrived(st.recv2.at[:, s], st.sem2[s])
        for way in range(2):
            i, sign, near = ring("y" if st.first == "x" else "x", way)
            c = mod4(i - (2 + s) * sign)
            total = st.recv2[way, s].astype(F32) + st.recv1[way, 2, c].astype(F32)
            st.recv2[way, s] = total.astype(BF16)
            if s < 2:
                wire.put(
                    st.recv2.at[way, s], st.recv2.at[way, s + 1], near, st.send2, st.sem2[s + 1]
                )
        if s == 2:
            wire.put(st.recv2.at[1 - zh, 2], st.recv3, z_far, st.send3, st.sem3)

    def result(st):
        wire.arrived(st.recv3, st.sem3)
        return (st.recv2[zh, 2].astype(F32) + st.recv3[...].astype(F32)).astype(BF16)

    def row_part(r0):
        def body(n, carry):
            cols = pl.ds(pl.multiple_of(n * 256, 256), 256)
            r = nt(gd[r0 : r0 + 256, :], wg[cols, :]) + nt(ud[r0 : r0 + 256, :], wu[cols, :])
            rg[r0 : r0 + 256, cols] = r.astype(BF16)
            return carry

        lax.fori_loop(0, D // 256, body, 0)

    rc_send, rc_far, rc_near = wire.group(rc), wire.sem(), wire.sem()
    rz_send, rz_in = wire.group(rz), wire.sem()
    cg_send, cg_sem = wire.group(cg_rows.at[pl.ds(1, 3)]), wire.sem()

    for j in range(4):
        pass_dy(j)
        wire.arrived(dy_block(3, j), dy_diag[j])
        down_part(d[j].partial, 512 * j)
        launch(d[j])
        hidden_part(256, j == 0, 512 * j, 512)
        if j == 0:
            turned(256)
        if j == 2:
            step1(d[0], 0)
            step1(d[1], 0)
    backward(256)
    up_part(g0.partial, gd, 0)
    launch(g0)
    up_part(g1.partial, gd, 384)
    launch(g1)
    step1(d[0], 1)
    step1(d[2], 0)
    step1(d[1], 1)
    step1(d[3], 0)
    up_part(u0.partial, ud, 0)
    launch(u0)
    up_part(u1.partial, ud, 384)
    launch(u1)
    step1(d[0], 2)
    step1(d[2], 1)
    step1(d[1], 2)
    step1(d[3], 1)
    row_part(256)
    wire.put(slot_rows(rg, 3), rc.at[1], mate, rc_send, rc_far)
    for slot in range(4):
        row = jnp.sum(jnp.transpose(cg_part[slot * T : slot * T + T, :]), axis=0, keepdims=True)
        cg_rows[slot] = jnp.broadcast_to(row, (8, T))
    for j, to in ((1, mate), (2, z_near), (3, z_diag)):
        wire.put(cg_rows.at[j], cg_in.at[j], to, cg_send, cg_sem)
    step1(g0, 0)
    step1(g1, 0)
    step1(d[2], 2)
    step1(d[3], 2)
    row_part(0)
    wire.put(slot_rows(rg, 1), rc.at[0], mate, rc_send, rc_near)
    step1(u0, 0)
    step1(u1, 0)
    wire.arrived(rc.at[1], rc_far)

    def add_far(i, carry):
        rows = pl.ds(pl.multiple_of(i * 16, 16), 16)
        full = pl.ds(pl.multiple_of(2 * T + i * 16, 16), 16)
        total = rg[full, :].astype(F32) + rc[1, rows, :].astype(F32)
        rg[full, :] = total.astype(BF16)
        return carry

    lax.fori_loop(0, T // 16, add_far, 0)
    wire.put(slot_rows(rg, 2), rz, z_near, rz_send, rz_in)

    step2(d[0], 0)
    step2(d[1], 0)
    step1(g0, 1)
    step1(g1, 1)
    step2(d[2], 0)
    step2(d[3], 0)
    step1(u0, 1)
    step1(u1, 1)

    wire.arrived(cg_in.at[pl.ds(1, 3)], cg_sem)
    answer = jnp.zeros((2, T), F32)
    for j in range(4):
        row = cg_rows[0, 0:1, :] if j == 0 else cg_in[j, 0:1, :]
        answer += jnp.where(ids_ref[...] == jnp.bitwise_xor(ex, j), row, 0.0)
    cg_out[...] = answer
    stores = [pltpu.make_async_copy(cg_out, cg_hbm, local_sem.at[5])]
    stores[0].start()

    for st in d:
        step2(st, 1)
    step1(g0, 2)
    step1(g1, 2)
    for st in d:
        step2(st, 2)
    step1(u0, 2)
    step1(u1, 2)
    step2(g0, 0)
    step2(g1, 0)

    wire.arrived(rc.at[0], rc_near)
    wire.arrived(rz, rz_in)

    def add_rows(i, carry):
        rows = pl.ds(pl.multiple_of(i * 16, 16), 16)
        total = rg[rows, :].astype(F32) + rc[0, rows, :].astype(F32) + rz[rows, :].astype(F32)
        ig_out[rows, :] = total.astype(BF16)
        return carry

    lax.fori_loop(0, T // 16, add_rows, 0)
    stores.append(pltpu.make_async_copy(ig_out, ig_hbm, local_sem.at[6]))
    stores[1].start()

    step2(u0, 0)
    step2(u1, 0)
    step2(g0, 1)
    step2(g1, 1)
    for j in range(4):
        dg_out[0, :, 512 * j : 512 * j + 512] = result(d[j])
    stores.append(pltpu.make_async_copy(dg_out, dg_hbm, local_sem.at[7]))
    stores[2].start()
    step2(u0, 1)
    step2(u1, 1)
    step2(g0, 2)
    step2(g1, 2)
    step2(u0, 2)
    step2(u1, 2)
    gg_out[0, :, 0:384] = result(g0)
    gg_out[0, :, 384:768] = result(g1)
    stores.append(pltpu.make_async_copy(gg_out, gg_hbm, local_sem.at[8]))
    stores[3].start()
    ug_out[0, :, 0:384] = result(u0)
    ug_out[0, :, 384:768] = result(u1)
    stores.append(pltpu.make_async_copy(ug_out, ug_hbm, local_sem.at[9]))
    stores[4].start()

    wire.finish()
    for store in stores:
        store.wait()


def hand_over(*refs):
    for src, dst in zip(refs[:5], refs[5:]):
        dst[...] = src[...]


OUTS = (
    jax.ShapeDtypeStruct((T, D), BF16),
    jax.ShapeDtypeStruct((2, T), F32),
    jax.ShapeDtypeStruct((1, 64, FF), BF16),
    jax.ShapeDtypeStruct((1, 64, FF), BF16),
    jax.ShapeDtypeStruct((1, 24, D), BF16),
)


def shards(tokens, cotangent, expert_ids, combine, w_gate, w_up, w_down):
    hbm = pl.BlockSpec(memory_space=pl.ANY)
    vmem = pl.BlockSpec(memory_space=pltpu.VMEM)
    outs = pl.pallas_call(
        kernel,
        out_shape=OUTS,
        in_specs=[hbm, hbm, vmem, vmem, hbm, hbm, hbm],
        out_specs=(hbm, hbm, hbm, hbm, hbm),
        scratch_shapes=[
            pltpu.VMEM((D, FF), BF16),
            pltpu.VMEM((D, FF), BF16),
            pltpu.VMEM((FF, D), BF16),
            pltpu.VMEM((4 * T, D), BF16),
            pltpu.VMEM((4 * T, D), BF16),
            pltpu.VMEM((D, 4 * T), BF16),
            pltpu.VMEM((256, FF), F32),
            pltpu.VMEM((256, FF), F32),
            pltpu.VMEM((256, FF), F32),
            pltpu.VMEM((256, FF), F32),
            pltpu.VMEM((256, FF), BF16),
            pltpu.VMEM((FF, 4 * T), BF16),
            pltpu.VMEM((4 * T, FF), BF16),
            pltpu.VMEM((4 * T, FF), BF16),
            pltpu.VMEM((4, 8, T), F32),
            pltpu.VMEM((4 * T, T), F32),
            pltpu.VMEM((4 * T, T), F32),
            pltpu.VMEM((4, 8, T), F32),
            pltpu.VMEM((4, 8, T), F32),
            pltpu.VMEM((4 * T, D), BF16),
            pltpu.VMEM((2, T, D), BF16),
            pltpu.VMEM((T, D), BF16),
            pltpu.VMEM((4, 4, 2, 4, 24, 512), BF16),
            pltpu.VMEM((4, 4, 2, 4, 64, 384), BF16),
            pltpu.VMEM((4, 2, 3, 4, 24, 512), BF16),
            pltpu.VMEM((4, 2, 3, 4, 64, 384), BF16),
            pltpu.VMEM((4, 2, 3, 24, 512), BF16),
            pltpu.VMEM((4, 2, 3, 64, 384), BF16),
            pltpu.VMEM((4, 24, 512), BF16),
            pltpu.VMEM((4, 64, 384), BF16),
            pltpu.VMEM((T, D), BF16),
            pltpu.VMEM((2, T), F32),
            pltpu.VMEM((1, 64, FF), BF16),
            pltpu.VMEM((1, 64, FF), BF16),
            pltpu.VMEM((1, 24, D), BF16),
            pltpu.SemaphoreType.DMA((10,)),
            pltpu.SemaphoreType.DMA((N_SEM,)),
        ],
        compiler_params=pltpu.CompilerParams(
            collective_id=0, has_side_effects=True, vmem_limit_bytes=60 * 1024 * 1024
        ),
        name="experts",
    )(tokens, cotangent, expert_ids.T, combine.T, w_gate, w_up, w_down)
    outs = pl.pallas_call(
        hand_over,
        out_shape=OUTS,
        in_specs=[vmem] * 5,
        out_specs=(vmem,) * 5,
        name="hand_over",
    )(*outs)
    return (outs[0], outs[1].T, *outs[2:])


def solution(mesh):
    both = ("dp", "expert")
    return jax.shard_map(
        shards,
        mesh=mesh,
        in_specs=(
            P(both, None),
            P(both, None),
            P(both, None),
            P(both, None),
            P("expert", None, None),
            P("expert", None, None),
            P("expert", None, None),
        ),
        out_specs=(
            P(both, None),
            P(both, None),
            P("expert", "dp", None),
            P("expert", "dp", None),
            P("expert", "dp", None),
        ),
        check_vma=False,
    )
```

time: 111 us -> 102 us (0.919)
  local copies, waits for them, and re-layouts: 10.8 us -> 0 us
  Pallas kernels: 99.5 us -> 101 us
    unnamed x6 -> x0, local copies, waits for them, and re-layouts: 9.32 us -> none
    pallas_call x1 -> x2, Pallas kernels: 99.5 us -> 101 us  [the longest x1 99.4 us: shards(): pl.pallas_call(kernel, out_shape=OUTS, in_specs=[hbm, hbm, vmem, vmem, hb...]
    pallas_call x1 -> x0, local copies, waits for them, and re-layouts: 1.48 us -> none  [shards(): pl.pallas_call(kernel, out_shape=(jax.ShapeDtypeStruct((T, D), BF16), jax...]
where the time goes in v2:
time: 102 us
  Pallas kernels  101 us (99%)
    pallas_call x1, Pallas kernels, shards(): pl.pallas_call(kernel, out_shape=OUTS, in_specs=[hbm, hbm, vmem, vmem, hb...  99.4 us

profile of v2, /device:TPU:0, one launch (start us, length us, event | category | flops | bytes accessed | tf_op | source)
XLA Modules:
  0.0 102.1 jit_solution(16582218856914406182)
XLA Ops:
  0.6 99.4 %experts.1 = (bf16[128,2048]{1,0:T(8,128)(2,1)}, f32[2,128]{1,0:T(2,128)}, bf16[1,64,768]{2,1,0:T(8,128)(2,1)}, bf16[1,64,768]{2,1,0:T(8,128)(2,1)}, bf16[1,24,2048]{2,1,0:T(8,128)(2,1)}) custom-call(bf16[128,2048]{1,0:T(8,128)(2,1)} %x_hbm.1, bf16[128,2048]{1,0:T(8,128)(2,1)} %dy_hbm.1, s32[2,128]{1,0:T(2,128)} %bitcast.3, f32[2,128]{1,0:T(2,128)} %bitcast.4, ...), custom_call_target="tpu_custom_call" | custom-call | tf_op jit(solution)/shard_map/experts/pallas_call | solution.py:523
  100.1 2.0 %hand_over.1 = (bf16[128,2048]{1,0:T(8,128)(2,1)}, f32[2,128]{1,0:T(2,128)}, bf16[1,64,768]{2,1,0:T(8,128)(2,1)}, bf16[1,64,768]{2,1,0:T(8,128)(2,1)}, bf16[1,24,2048]{2,1,0:T(8,128)(2,1)}) custom-call(bf16[128,2048]{1,0:T(8,128)(2,1)} %get-tuple-element.15.refs_0_, f32[2,128]{1,0:T(2,128)} %get-tuple-element.16.refs_1_, ...), custom_call_target="tpu_custom_call" | custom-call | tf_op jit(solution)/shard_map/hand_over/pallas_call | solution.py:572

commit v3 on v2

v3 whole, which is shorter than its diff:
```python
import jax
import jax.numpy as jnp
from jax import lax
from jax.experimental import pallas as pl
from jax.experimental.pallas import tpu as pltpu
from jax.sharding import PartitionSpec as P

MESH = pl.DeviceIdType.MESH
BF16 = jnp.bfloat16
F32 = jnp.float32
D = 2048
FF = 768
T = 128
N_SEM = 150


def mod4(v):
    return lax.rem(v + 8, 4)


def nt(a, b):
    return lax.dot_general(a, b, (((1,), (1,)), ((), ())), preferred_element_type=F32)


def nn(a, b):
    return jnp.dot(a, b, preferred_element_type=F32)


class Wire:
    def __init__(self, sems, other):
        self.sems, self.other, self.count, self.groups = sems, other, 0, []

    def sem(self):
        self.count += 1
        return self.sems.at[self.count - 1]

    def describe(self, src, dst, send, recv, device):
        return pltpu.make_async_remote_copy(
            src_ref=src,
            dst_ref=dst,
            send_sem=send,
            recv_sem=recv,
            device_id=device,
            device_id_type=MESH,
        )

    def group(self, total):
        send = self.sem()
        self.groups.append((send, total))
        return send

    def put(self, src, dst, device, send, recv):
        self.describe(src, dst, send, recv, device).start()

    def arrived(self, ref, recv):
        self.describe(ref, ref, recv, recv, self.other).wait_recv()

    def finish(self):
        for send, total in self.groups:
            self.describe(total, total, send, send, self.other).wait_send()


class Sums:
    def __init__(self, right, out, parts, store):
        self.right, self.out, self.parts, self.store = right, out, parts, store

    def put(self, rows, c0, value):
        self.out[0, rows, c0 : c0 + value.shape[1]] = value.astype(BF16)

    def count(self):
        self.parts -= 1
        if self.parts == 0:
            self.store()


class Stream:
    def __init__(self, wire, first, partial, recv1, recv2, recv3, sends, sums, c0, far=False):
        self.first, self.partial, self.far = first, partial, far
        self.second = "y" if first == "x" else "x"
        self.sums, self.c0 = sums, c0
        self.recv1, self.recv2, self.recv3 = recv1, recv2, recv3
        self.send1, self.send2, self.send3 = sends
        self.sem1 = [wire.sem() for _ in range(2)]
        self.sem2 = [wire.sem() for _ in range(2)]
        self.sem3 = wire.sem()

    def chunk(self, way, c):
        if self.far:
            rows = pl.ds(32 * way, 32)
            return (c, slice(None), rows) if self.first == "x" else (slice(None), c, rows)
        return (c, way) if self.first == "x" else (slice(None), way, c)

    def own(self, way, c, j):
        x, y = (c, j) if self.first == "x" else (j, c)
        if self.far:
            return self.recv3[x, y, 32 * way : 32 * way + 32]
        return self.partial[x, way, y]


def kernel(
    x_hbm,
    dy_hbm,
    ids_ref,
    comb_ref,
    wg_hbm,
    wu_hbm,
    wd_hbm,
    ig_hbm,
    cg_hbm,
    gg_hbm,
    ug_hbm,
    dg_hbm,
    wg,
    wu,
    wd,
    x,
    dy,
    xt,
    act,
    dact,
    hid,
    hg,
    hc,
    hct,
    gd,
    ud,
    weight_rows,
    weight_cols,
    cg_part,
    cg_rows,
    cg_in,
    rg,
    rc,
    rz,
    pd,
    pg,
    pz,
    rd1,
    rg1,
    rz1,
    rd2,
    rg2,
    rz2,
    rd3,
    rg3,
    rz3,
    ig_out,
    cg_out,
    gg_out,
    ug_out,
    dg_out,
    local_sem,
    remote_sem,
):
    dp, ex = lax.axis_index("dp"), lax.axis_index("expert")
    ix, zh, iy = lax.div(dp, 8), lax.rem(lax.div(dp, 4), 2), lax.rem(dp, 4)
    zl, core = lax.div(ex, 2), lax.rem(ex, 2)

    def at(a, b, c):
        return {"dp": a * 8 + b * 4 + c, "expert": ex}

    x_next, x_prev = at(mod4(ix + 1), zh, iy), at(mod4(ix - 1), zh, iy)
    y_next, y_prev = at(ix, zh, mod4(iy + 1)), at(ix, zh, mod4(iy - 1))
    z_far = at(ix, 1 - zh, iy)
    mate = {"dp": dp, "expert": zl * 2 + 1 - core}
    z_near = {"dp": dp, "expert": (1 - zl) * 2 + core}
    z_diag = {"dp": dp, "expert": (1 - zl) * 2 + 1 - core}

    loads = [
        pltpu.make_async_copy(x_hbm, x.at[pl.ds(0, T)], local_sem.at[0]),
        pltpu.make_async_copy(dy_hbm, dy.at[pl.ds(0, T)], local_sem.at[1]),
        pltpu.make_async_copy(wg_hbm.at[0], wg, local_sem.at[2]),
        pltpu.make_async_copy(wu_hbm.at[0], wu, local_sem.at[3]),
        pltpu.make_async_copy(wd_hbm.at[0], wd, local_sem.at[4]),
    ]
    for load in loads:
        load.start()

    barrier = pltpu.get_barrier_semaphore()
    peers = (x_next, x_prev, y_next, y_prev, z_far, mate, z_near, z_diag)
    for peer in peers:
        pl.semaphore_signal(barrier, inc=1, device_id=peer, device_id_type=MESH)
    pl.semaphore_wait(barrier, len(peers))

    wire = Wire(remote_sem, mate)

    def slot_rows(ref, slot):
        return ref.at[pl.ds(slot * T, T)]

    def x_block(slot, j):
        return x.at[pl.ds(slot * T + 64 * j, 64)]

    def dy_block(slot, j):
        return dy.at[pl.ds(slot * T, T), pl.ds(256 * j, 256)]

    x_near_send, x_near = wire.group(slot_rows(x, 0)), [wire.sem() for _ in range(2)]
    x_mate_send, x_mate = wire.group(slot_rows(x, 0)), wire.sem()
    x_pass_send, x_diag = wire.group(slot_rows(x, 2)), [wire.sem() for _ in range(2)]
    dy_near_send, dy_near = wire.group(slot_rows(dy, 0)), [wire.sem() for _ in range(8)]
    dy_mate_send, dy_mate = wire.group(slot_rows(dy, 0)), wire.sem()
    dy_pass_send, dy_diag = wire.group(slot_rows(dy, 2)), [wire.sem() for _ in range(8)]
    w_send, w_in = wire.group(weight_rows.at[pl.ds(1, 3)]), wire.sem()

    expert = lax.broadcasted_iota(jnp.int32, (8, T), 0)
    dense = jnp.zeros((8, T), F32)
    for k in range(2):
        dense += jnp.where(ids_ref[k : k + 1, :] == expert, comb_ref[k : k + 1, :], 0.0)
    weight_rows[0] = dense
    for j, to in ((1, mate), (2, z_near), (3, z_diag)):
        wire.put(weight_rows.at[0], weight_rows.at[j], to, w_send, w_in)

    loads[0].wait()
    for j in range(2):
        wire.put(x_block(0, j), x_block(2, j), z_near, x_near_send, x_near[j])
    wire.put(slot_rows(x, 0), slot_rows(x, 1), mate, x_mate_send, x_mate)
    loads[1].wait()
    for j in range(8):
        wire.put(dy_block(0, j), dy_block(2, j), z_near, dy_near_send, dy_near[j])
    wire.put(slot_rows(dy, 0), slot_rows(dy, 1), mate, dy_mate_send, dy_mate)

    def pass_x(j):
        wire.arrived(x_block(2, j), x_near[j])
        wire.put(x_block(2, j), x_block(3, j), mate, x_pass_send, x_diag[j])

    def pass_dy(j):
        wire.arrived(dy_block(2, j), dy_near[j])
        wire.put(dy_block(2, j), dy_block(3, j), mate, dy_pass_send, dy_diag[j])

    def column_weights(slot):
        row = weight_rows[slot, pl.ds(ex, 1), :]
        weight_cols[slot * T : slot * T + T, :] = jnp.transpose(jnp.broadcast_to(row, (T, T)))

    def spread(start):
        col = weight_cols[pl.ds(start, 16), :]
        return jnp.concatenate([col] * 6, axis=1)

    def turned(r0):
        def body(j, carry):
            cols = pl.ds(pl.multiple_of(j * 256, 256), 256)
            xt[cols, r0 : r0 + 256] = jnp.transpose(x[r0 : r0 + 256, cols])
            return carry

        lax.fori_loop(0, D // 256, body, 0)

    def gated(rows, start):
        gate, up = act[rows, :], dact[rows, :]
        s = jax.nn.sigmoid(gate)
        a = gate * s
        h = a * up
        act[rows, :] = a
        dact[rows, :] = up * s * (1.0 + gate * (1.0 - s))
        hid[rows, :] = h
        hc[rows, :] = (h * spread(start)).astype(BF16)

    def hidden_turned(r0):
        def turn(n, carry):
            cols = pl.ds(pl.multiple_of(n * 256, 256), 256)
            hct[cols, r0 : r0 + 256] = jnp.transpose(hc[:, cols])
            return carry

        lax.fori_loop(0, FF // 256, turn, 0)

    def forward():
        def matmul(n, carry):
            cols = pl.ds(pl.multiple_of(n * 256, 256), 256)
            act[:, cols] = nn(x[0:256, :], wg[:, cols])
            dact[:, cols] = nn(x[0:256, :], wu[:, cols])
            return carry

        lax.fori_loop(0, FF // 256, matmul, 0)

        def pointwise(i, carry):
            start = pl.multiple_of(i * 16, 16)
            gated(pl.ds(start, 16), start)
            return carry

        lax.fori_loop(0, 16, pointwise, 0)
        hidden_turned(0)

    def other_matmul(b):
        def matmul(n, carry):
            cols = pl.ds(pl.multiple_of(n * 256, 256), 256)
            starts = (2 * T + 64 * b, 3 * T + 64 * b)
            left = jnp.concatenate([x[r : r + 64, :] for r in starts], axis=0)
            for out, w in ((act, wg), (dact, wu)):
                r = nn(left, w[:, cols])
                out[64 * b : 64 * b + 64, cols] = r[0:64]
                out[T + 64 * b : T + 64 * b + 64, cols] = r[64:128]
            return carry

        lax.fori_loop(0, FF // 256, matmul, 0)

    def other_pointwise(b):
        def pointwise(i, carry):
            start = 64 * b + T * lax.div(i, 4) + 16 * lax.rem(i, 4)
            start = pl.multiple_of(start, 16)
            gated(pl.ds(start, 16), pl.multiple_of(256 + start, 16))
            return carry

        lax.fori_loop(0, 8, pointwise, 0)
        if b == 1:
            hidden_turned(256)

    def hidden_part(r0, first, j0, width):
        def matmul(n, carry):
            cols = pl.ds(pl.multiple_of(n * 256, 256), 256)
            r = nt(dy[r0 : r0 + 256, j0 : j0 + width], wd[cols, j0 : j0 + width])
            hg[:, cols] = r if first else hg[:, cols] + r
            return carry

        lax.fori_loop(0, FF // 256, matmul, 0)

    def backward(r0):
        def pointwise(i, carry):
            rows = pl.ds(pl.multiple_of(i * 16, 16), 16)
            full = pl.ds(pl.multiple_of(r0 + i * 16, 16), 16)
            g = hg[rows, :]
            prod = g * hid[rows, :]
            total = prod[:, 0:128]
            for j in range(1, 6):
                total += prod[:, 128 * j : 128 * j + 128]
            cg_part[full, :] = total
            g = g * spread(pl.multiple_of(r0 + i * 16, 16))
            gd[full, :] = (g * dact[rows, :]).astype(BF16)
            ud[full, :] = (g * act[rows, :]).astype(BF16)
            return carry

        lax.fori_loop(0, 16, pointwise, 0)

    loads[2].wait()
    loads[3].wait()
    wire.arrived(slot_rows(x, 1), x_mate)
    wire.arrived(weight_rows.at[pl.ds(1, 3)], w_in)
    for slot in range(4):
        column_weights(slot)
    forward()
    pass_x(0)
    turned(0)
    loads[4].wait()
    wire.arrived(slot_rows(dy, 1), dy_mate)
    hidden_part(0, True, 0, D)
    backward(0)
    wire.arrived(x_block(3, 0), x_diag[0])
    other_matmul(0)
    pass_x(1)
    other_pointwise(0)
    wire.arrived(x_block(3, 1), x_diag[1])

    stores = []

    def store(src, dst):
        stores.append(pltpu.make_async_copy(src, dst, local_sem.at[5 + len(stores)]))
        stores[-1].start()

    down = Sums(None, dg_out, 8, lambda: store(dg_out, dg_hbm))
    gate = Sums(gd, gg_out, 4, lambda: store(gg_out, gg_hbm))
    upper = Sums(ud, ug_out, 4, lambda: store(ug_out, ug_hbm))
    d_sends = [wire.group(ref) for ref in (rd1, rd2, rd3)]
    g_sends = [wire.group(ref) for ref in (rg1, rg2, rg3)]
    z_sends = [wire.group(ref) for ref in (rz1, rz2, rz3)]
    def axis(j):
        return "xy"[j % 2]

    d = [
        Stream(wire, axis(j), pd.at[j], rd1.at[j], rd2.at[j], rd3.at[j], d_sends, down, 256 * j)
        for j in range(8)
    ]
    up = [
        Stream(wire, axis(j), pg.at[j], rg1.at[j], rg2.at[j], rg3.at[j], g_sends, sums, 256 * (j % 2))
        for j, sums in enumerate((gate, gate, upper, upper))
    ]
    far = [
        Stream(wire, axis(j), pz.at[j], rz1.at[j], rz2.at[j], rz3.at[j], z_sends, sums, c0, True)
        for j, (sums, c0) in enumerate(((gate, 512), (gate, 640), (upper, 512), (upper, 640)))
    ]

    def ring(first, way):
        i = ix if first == "x" else iy
        near = (x_next, x_prev) if first == "x" else (y_next, y_prev)
        return i, 1 - 2 * way, near[way], near[1 - way]

    def launch_relay(st):
        source = st.recv3 if st.far else st.partial
        for way in range(2):
            i, sign, ahead, behind = ring(st.first, way)
            src = source.at[st.chunk(way, mod4(i + 2))]
            wire.put(src, st.recv1.at[way, 0], behind, st.send1, st.sem1[0])

    def launch_direct(st):
        source = st.recv3 if st.far else st.partial
        for way in range(2):
            i, sign, ahead, behind = ring(st.first, way)
            src = source.at[st.chunk(way, mod4(i + sign))]
            wire.put(src, st.recv1.at[way, 1], ahead, st.send1, st.sem1[1])

    def launch(st):
        launch_relay(st)
        launch_direct(st)

    def down_part(j):
        wire.arrived(dy_block(3, j), dy_diag[j])
        r = nn(hct[...], dy[:, 256 * j : 256 * j + 256]).reshape(4, 2, 4, 24, 256)
        pd[j] = r.astype(BF16)
        launch(d[j])

    def up_chunk(st, away):
        right, c0 = st.sums.right, st.c0
        for way in range(2):
            i, sign, ahead, behind = ring(st.first, way)
            c = mod4(i + away * sign)
            if st.first == "x":
                rows = pl.multiple_of(c * 512 + way * 256, 256)
                left = xt[pl.ds(rows, 256), :]
            else:
                starts = [pl.multiple_of(j * 512 + way * 256 + c * 64, 64) for j in range(4)]
                left = jnp.concatenate([xt[pl.ds(r, 64), :] for r in starts], axis=0)
            r = nn(left, right[:, c0 : c0 + 256]).astype(BF16).reshape(4, 64, 256)
            if st.first == "x":
                st.partial[c, way] = r
            else:
                for j in range(4):
                    st.partial[j, way, c] = r[j]

    def up_first(st):
        up_chunk(st, 2)
        launch_relay(st)

    def up_rest(st):
        up_chunk(st, 1)
        launch_direct(st)

        up_chunk(st, -1)
        up_chunk(st, 0)

    def far_part(kind, half):
        right, k = (gd, ud)[kind], 2 * kind

        def body(c, carry):
            rows = pl.multiple_of(c * 512 + half * 256, 256)
            r = nn(xt[pl.ds(rows, 256), :], right[:, 512:768]).astype(BF16)
            r = r.reshape(4, 64, 256)
            pz[k, c, half] = r[:, :, 0:128]
            pz[k + 1, c, half] = r[:, :, 128:256]
            return carry

        lax.fori_loop(0, 4, body, 0)

    def far_first(kind):
        far_part(kind, 1 - zh)
        for st in far[2 * kind : 2 * kind + 2]:
            wire.put(st.partial.at[:, 1 - zh], st.recv3, z_far, st.send3, st.sem3)

    def far_sum(st):
        wire.arrived(st.recv3, st.sem3)

        def body(c, carry):
            for j in range(4):
                total = st.recv3[c, j].astype(F32) + st.partial[c, zh, j].astype(F32)
                st.recv3[c, j] = total.astype(BF16)
            return carry

        lax.fori_loop(0, 4, body, 0)
        launch(st)

    def step1(st, s):
        if s == 0:
            wire.arrived(st.recv1.at[:, 0], st.sem1[0])
        else:
            wire.arrived(st.recv1.at[:, pl.ds(1, 2)], st.sem1[1])
        for way in range(2):
            i, sign, ahead, behind = ring(st.first, way)
            c = mod4(i - sign) if s == 0 else i
            for j in range(4):
                total = st.recv1[way, s, j].astype(F32) + st.own(way, c, j).astype(F32)
                if s == 1:
                    total += st.recv1[way, 2, j].astype(F32)
                st.recv1[way, 2 * s, j] = total.astype(BF16)
            if s == 0:
                wire.put(st.recv1.at[way, 0], st.recv1.at[way, 2], behind, st.send1, st.sem1[1])
        if s == 1:
            for way in range(2):
                i, sign, ahead, behind = ring(st.second, way)
                src = st.recv1.at[way, 2, mod4(i + 2)]
                wire.put(src, st.recv2.at[way, 0], behind, st.send2, st.sem2[0])
            for way in range(2):
                i, sign, ahead, behind = ring(st.second, way)
                src = st.recv1.at[way, 2, mod4(i + sign)]
                wire.put(src, st.recv2.at[way, 1], ahead, st.send2, st.sem2[1])

    def step2(st, s):
        if s == 0:
            wire.arrived(st.recv2.at[:, 0], st.sem2[0])
        else:
            wire.arrived(st.recv2.at[:, pl.ds(1, 2)], st.sem2[1])
        for way in range(2):
            i, sign, ahead, behind = ring(st.second, way)
            c = mod4(i - sign) if s == 0 else i
            total = st.recv2[way, s].astype(F32) + st.recv1[way, 2, c].astype(F32)
            if s == 0:
                st.recv2[way, 0] = total.astype(BF16)
                wire.put(st.recv2.at[way, 0], st.recv2.at[way, 2], behind, st.send2, st.sem2[1])
                continue
            total += st.recv2[way, 2].astype(F32)
            if st.far:
                st.sums.put(slice(32 * way, 32 * way + 32), st.c0, total)
            else:
                st.recv2[way, 2] = total.astype(BF16)
        if s == 1 and st.far:
            st.sums.count()
        elif s == 1:
            wire.put(st.recv2.at[1 - zh, 2], st.recv3, z_far, st.send3, st.sem3)

    def result(st):
        wire.arrived(st.recv3, st.sem3)
        total = st.recv2[zh, 2].astype(F32) + st.recv3[...].astype(F32)
        st.sums.put(slice(None), st.c0, total)
        st.sums.count()

    rc_send, rc_far, rc_near = wire.group(rc), wire.sem(), wire.sem()
    rz_send, rz_in = wire.group(rz), wire.sem()
    cg_send, cg_sem = wire.group(cg_rows.at[pl.ds(1, 3)]), wire.sem()

    def row_part(half, q):
        r0 = 256 * half

        def body(n, carry):
            cols = pl.ds(pl.multiple_of(q * 512 + n * 256, 256), 256)
            r = nt(gd[r0 : r0 + 256, :], wg[cols, :]) + nt(ud[r0 : r0 + 256, :], wu[cols, :])
            rg[r0 : r0 + 256, cols] = r.astype(BF16)
            return carry

        lax.fori_loop(0, 2, body, 0)
        if q == 3:
            if half == 1:
                wire.put(slot_rows(rg, 3), rc.at[1], mate, rc_send, rc_far)
            else:
                wire.put(slot_rows(rg, 1), rc.at[0], mate, rc_send, rc_near)

    def add_far():
        wire.arrived(rc.at[1], rc_far)

        def body(i, carry):
            rows = pl.ds(pl.multiple_of(i * 16, 16), 16)
            full = pl.ds(pl.multiple_of(2 * T + i * 16, 16), 16)
            total = rg[full, :].astype(F32) + rc[1, rows, :].astype(F32)
            rg[full, :] = total.astype(BF16)
            return carry

        lax.fori_loop(0, T // 16, body, 0)
        wire.put(slot_rows(rg, 2), rz, z_near, rz_send, rz_in)

    def add_rows():
        wire.arrived(rc.at[0], rc_near)
        wire.arrived(rz, rz_in)

        def body(i, carry):
            rows = pl.ds(pl.multiple_of(i * 16, 16), 16)
            total = rg[rows, :].astype(F32) + rc[0, rows, :].astype(F32)
            ig_out[rows, :] = (total + rz[rows, :].astype(F32)).astype(BF16)
            return carry

        lax.fori_loop(0, T // 16, body, 0)
        store(ig_out, ig_hbm)

    def combine_part():
        for slot in range(4):
            part = jnp.transpose(cg_part[slot * T : slot * T + T, :])
            cg_rows[slot] = jnp.broadcast_to(jnp.sum(part, axis=0, keepdims=True), (8, T))
        for j, to in ((1, mate), (2, z_near), (3, z_diag)):
            wire.put(cg_rows.at[j], cg_in.at[j], to, cg_send, cg_sem)

    def combine_result():
        wire.arrived(cg_in.at[pl.ds(1, 3)], cg_sem)
        answer = jnp.zeros((2, T), F32)
        for j in range(4):
            row = cg_rows[0, 0:1, :] if j == 0 else cg_in[j, 0:1, :]
            answer += jnp.where(ids_ref[...] == jnp.bitwise_xor(ex, j), row, 0.0)
        cg_out[...] = answer
        store(cg_out, cg_hbm)

    other_matmul(1)
    pass_dy(0)
    pass_dy(1)
    other_pointwise(1)
    turned(256)
    pass_dy(2)
    pass_dy(3)
    down_part(0)
    down_part(1)
    hidden_part(256, True, 0, 512)
    pass_dy(4)
    down_part(2)
    down_part(3)
    pass_dy(5)
    hidden_part(256, False, 512, 512)
    down_part(4)
    pass_dy(6)
    step1(d[0], 0)
    down_part(5)
    pass_dy(7)
    step1(d[1], 0)
    hidden_part(256, False, 1024, 512)
    down_part(6)
    step1(d[2], 0)
    step1(d[3], 0)
    down_part(7)
    hidden_part(256, False, 1536, 512)
    step1(d[4], 0)
    backward(256)
    far_first(0)
    step1(d[5], 0)
    up_first(up[0])
    up_first(up[2])
    up_first(up[3])
    far_first(1)
    step1(d[6], 0)
    step1(d[1], 1)
    up_first(up[1])
    far_part(0, zh)
    step1(d[3], 1)
    up_rest(up[2])
    step1(d[2], 1)
    step1(d[7], 0)
    far_part(1, zh)
    up_rest(up[1])
    step1(d[5], 1)
    up_rest(up[3])
    row_part(1, 0)
    combine_part()
    row_part(1, 1)
    step1(up[3], 0)
    row_part(1, 2)
    far_sum(far[0])
    row_part(1, 3)
    step1(up[2], 0)
    row_part(0, 0)
    step1(up[1], 0)
    row_part(0, 1)
    step2(d[1], 0)
    step2(d[2], 0)
    step2(d[3], 0)
    row_part(0, 2)
    step1(d[7], 1)
    add_far()
    row_part(0, 3)
    up_rest(up[0])
    step1(up[0], 0)
    step1(d[0], 1)
    step1(d[4], 1)
    step1(d[6], 1)
    far_sum(far[1])
    step2(d[5], 0)
    step1(far[0], 0)
    step1(up[2], 1)
    step2(d[1], 1)
    step2(d[3], 1)
    far_sum(far[2])
    step2(d[7], 0)
    step1(up[3], 1)
    step1(up[1], 1)
    step2(d[2], 1)
    step2(d[0], 0)
    step2(d[4], 0)
    step2(d[6], 0)
    far_sum(far[3])
    step1(up[0], 1)
    step1(far[1], 0)
    step2(d[5], 1)
    step1(far[0], 1)
    step2(up[2], 0)
    step1(far[2], 0)
    step2(d[0], 1)
    step2(d[7], 1)
    step2(d[4], 1)
    step2(d[6], 1)
    step2(up[3], 0)
    step1(far[3], 0)
    step2(up[1], 0)
    step2(up[0], 0)
    step1(far[2], 1)
    step1(far[1], 1)
    step2(far[0], 0)
    step2(up[3], 1)
    step2(up[2], 1)
    step1(far[3], 1)
    step2(up[1], 1)
    add_rows()
    step2(up[0], 1)
    combine_result()
    step2(far[2], 0)
    step2(far[1], 0)
    step2(far[0], 1)
    result(d[1])
    result(d[3])
    result(d[2])
    step2(far[3], 0)
    result(d[5])
    result(d[0])
    result(d[7])
    result(d[4])
    result(d[6])
    step2(far[2], 1)
    step2(far[1], 1)
    result(up[3])
    result(up[2])
    result(up[1])
    step2(far[3], 1)
    result(up[0])

    wire.finish()
    for store in stores:
        store.wait()


def hand_over(*refs):
    for src, dst in zip(refs[:5], refs[5:]):
        dst[...] = src[...]


OUTS = (
    jax.ShapeDtypeStruct((T, D), BF16),
    jax.ShapeDtypeStruct((2, T), F32),
    jax.ShapeDtypeStruct((1, 64, FF), BF16),
    jax.ShapeDtypeStruct((1, 64, FF), BF16),
    jax.ShapeDtypeStruct((1, 24, D), BF16),
)


def shards(tokens, cotangent, expert_ids, combine, w_gate, w_up, w_down):
    hbm = pl.BlockSpec(memory_space=pl.ANY)
    vmem = pl.BlockSpec(memory_space=pltpu.VMEM)
    outs = pl.pallas_call(
        kernel,
        out_shape=OUTS,
        in_specs=[hbm, hbm, vmem, vmem, hbm, hbm, hbm],
        out_specs=(hbm, hbm, hbm, hbm, hbm),
        scratch_shapes=[
            pltpu.VMEM((D, FF), BF16),
            pltpu.VMEM((D, FF), BF16),
            pltpu.VMEM((FF, D), BF16),
            pltpu.VMEM((4 * T, D), BF16),
            pltpu.VMEM((4 * T, D), BF16),
            pltpu.VMEM((D, 4 * T), BF16),
            pltpu.VMEM((256, FF), F32),
            pltpu.VMEM((256, FF), F32),
            pltpu.VMEM((256, FF), F32),
            pltpu.VMEM((256, FF), F32),
            pltpu.VMEM((256, FF), BF16),
            pltpu.VMEM((FF, 4 * T), BF16),
            pltpu.VMEM((4 * T, FF), BF16),
            pltpu.VMEM((4 * T, FF), BF16),
            pltpu.VMEM((4, 8, T), F32),
            pltpu.VMEM((4 * T, T), F32),
            pltpu.VMEM((4 * T, T), F32),
            pltpu.VMEM((4, 8, T), F32),
            pltpu.VMEM((4, 8, T), F32),
            pltpu.VMEM((4 * T, D), BF16),
            pltpu.VMEM((2, T, D), BF16),
            pltpu.VMEM((T, D), BF16),
            pltpu.VMEM((8, 4, 2, 4, 24, 256), BF16),
            pltpu.VMEM((4, 4, 2, 4, 64, 256), BF16),
            pltpu.VMEM((4, 4, 2, 4, 64, 128), BF16),
            pltpu.VMEM((8, 2, 3, 4, 24, 256), BF16),
            pltpu.VMEM((4, 2, 3, 4, 64, 256), BF16),
            pltpu.VMEM((4, 2, 3, 4, 32, 128), BF16),
            pltpu.VMEM((8, 2, 3, 24, 256), BF16),
            pltpu.VMEM((4, 2, 3, 64, 256), BF16),
            pltpu.VMEM((4, 2, 3, 32, 128), BF16),
            pltpu.VMEM((8, 24, 256), BF16),
            pltpu.VMEM((4, 64, 256), BF16),
            pltpu.VMEM((4, 4, 4, 64, 128), BF16),
            pltpu.VMEM((T, D), BF16),
            pltpu.VMEM((2, T), F32),
            pltpu.VMEM((1, 64, FF), BF16),
            pltpu.VMEM((1, 64, FF), BF16),
            pltpu.VMEM((1, 24, D), BF16),
            pltpu.SemaphoreType.DMA((10,)),
            pltpu.SemaphoreType.DMA((N_SEM,)),
        ],
        compiler_params=pltpu.CompilerParams(
            collective_id=0, has_side_effects=True, vmem_limit_bytes=60 * 1024 * 1024
        ),
        name="experts",
    )(tokens, cotangent, expert_ids.T, combine.T, w_gate, w_up, w_down)
    outs = pl.pallas_call(
        hand_over,
        out_shape=OUTS,
        in_specs=[vmem] * 5,
        out_specs=(vmem,) * 5,
        name="hand_over",
    )(*outs)
    return (outs[0], outs[1].T, *outs[2:])


def solution(mesh):
    both = ("dp", "expert")
    return jax.shard_map(
        shards,
        mesh=mesh,
        in_specs=(
            P(both, None),
            P(both, None),
            P(both, None),
            P(both, None),
            P("expert", None, None),
            P("expert", None, None),
            P("expert", None, None),
        ),
        out_specs=(
            P(both, None),
            P(both, None),
            P("expert", "dp", None),
            P("expert", "dp", None),
            P("expert", "dp", None),
        ),
        check_vma=False,
    )
```

time: 102 us -> 82.8 us (0.81)
  Pallas kernels: 101 us -> 82 us
    pallas_call x1, Pallas kernels: 99.4 us -> 80 us  [shards(): pl.pallas_call(kernel, out_shape=OUTS, in_specs=[hbm, hbm, vmem, vmem, hb...]
where the time goes in v3:
time: 82.8 us; the launch traced here: 82.7 us
  Pallas kernels  82 us (99%)
    pallas_call x1, Pallas kernels, shards(): pl.pallas_call(kernel, out_shape=OUTS, in_specs=[hbm, hbm, vmem, vmem, hb...  80 us
    pallas_call x1, Pallas kernels, shards(): pl.pallas_call(hand_over, out_shape=OUTS, in_specs=[vmem] * 5, out_specs=...  2.03 us

profile of v3, /device:TPU:0, one launch (start us, length us, event | category | flops | bytes accessed | tf_op | source)
XLA Modules:
  0.0 82.7 jit_solution(8626961794521750474)
XLA Ops:
  0.6 80.0 %experts.1 = (bf16[128,2048]{1,0:T(8,128)(2,1)}, f32[2,128]{1,0:T(2,128)}, bf16[1,64,768]{2,1,0:T(8,128)(2,1)}, bf16[1,64,768]{2,1,0:T(8,128)(2,1)}, bf16[1,24,2048]{2,1,0:T(8,128)(2,1)}) custom-call(bf16[128,2048]{1,0:T(8,128)(2,1)} %x_hbm.1, bf16[128,2048]{1,0:T(8,128)(2,1)} %dy_hbm.1, s32[2,128]{1,0:T(2,128)} %bitcast.3, f32[2,128]{1,0:T(2,128)} %bitcast.4, ...), custom_call_target="tpu_custom_call" | custom-call | tf_op jit(solution)/shard_map/experts/pallas_call | solution.py:732
  80.6 2.0 %hand_over.1 = (bf16[128,2048]{1,0:T(8,128)(2,1)}, f32[2,128]{1,0:T(2,128)}, bf16[1,64,768]{2,1,0:T(8,128)(2,1)}, bf16[1,64,768]{2,1,0:T(8,128)(2,1)}, bf16[1,24,2048]{2,1,0:T(8,128)(2,1)}) custom-call(bf16[128,2048]{1,0:T(8,128)(2,1)} %get-tuple-element.15.refs_0_, f32[2,128]{1,0:T(2,128)} %get-tuple-element.16.refs_1_, ...), custom_call_target="tpu_custom_call" | custom-call | tf_op jit(solution)/shard_map/hand_over/pallas_call | solution.py:785

commit v4 on v3

--- a/solution.py
+++ b/solution.py
@@ -61,16 +61,11 @@
 
 
 class Sums:
-    def __init__(self, right, out, parts, store):
-        self.right, self.out, self.parts, self.store = right, out, parts, store
+    def __init__(self, right, out):
+        self.right, self.out = right, out
 
     def put(self, rows, c0, value):
         self.out[0, rows, c0 : c0 + value.shape[1]] = value.astype(BF16)
-
-    def count(self):
-        self.parts -= 1
-        if self.parts == 0:
-            self.store()
 
 
 class Stream:
@@ -105,11 +100,11 @@
     wg_hbm,
     wu_hbm,
     wd_hbm,
-    ig_hbm,
-    cg_hbm,
-    gg_hbm,
-    ug_hbm,
-    dg_hbm,
+    ig_out,
+    cg_out,
+    gg_out,
+    ug_out,
+    dg_out,
     wg,
     wu,
     wd,
@@ -144,11 +139,6 @@
     rd3,
     rg3,
     rz3,
-    ig_out,
-    cg_out,
-    gg_out,
-    ug_out,
-    dg_out,
     local_sem,
     remote_sem,
 ):
@@ -344,17 +334,12 @@
     other_matmul(0)
     pass_x(1)
     other_pointwise(0)
+    pass_dy(0)
     wire.arrived(x_block(3, 1), x_diag[1])
 
-    stores = []
-
-    def store(src, dst):
-        stores.append(pltpu.make_async_copy(src, dst, local_sem.at[5 + len(stores)]))
-        stores[-1].start()
-
-    down = Sums(None, dg_out, 8, lambda: store(dg_out, dg_hbm))
-    gate = Sums(gd, gg_out, 4, lambda: store(gg_out, gg_hbm))
-    upper = Sums(ud, ug_out, 4, lambda: store(ug_out, ug_hbm))
+    down = Sums(None, dg_out)
+    gate = Sums(gd, gg_out)
+    upper = Sums(ud, ug_out)
     d_sends = [wire.group(ref) for ref in (rd1, rd2, rd3)]
     g_sends = [wire.group(ref) for ref in (rg1, rg2, rg3)]
     z_sends = [wire.group(ref) for ref in (rz1, rz2, rz3)]
@@ -505,16 +490,13 @@
                 st.sums.put(slice(32 * way, 32 * way + 32), st.c0, total)
             else:
                 st.recv2[way, 2] = total.astype(BF16)
-        if s == 1 and st.far:
-            st.sums.count()
-        elif s == 1:
+        if s == 1 and not st.far:
             wire.put(st.recv2.at[1 - zh, 2], st.recv3, z_far, st.send3, st.sem3)
 
     def result(st):
         wire.arrived(st.recv3, st.sem3)
         total = st.recv2[zh, 2].astype(F32) + st.recv3[...].astype(F32)
         st.sums.put(slice(None), st.c0, total)
-        st.sums.count()
 
     rc_send, rc_far, rc_near = wire.group(rc), wire.sem(), wire.sem()
     rz_send, rz_in = wire.group(rz), wire.sem()
@@ -560,7 +542,6 @@
             return carry
 
         lax.fori_loop(0, T // 16, body, 0)
-        store(ig_out, ig_hbm)
 
     def combine_part():
         for slot in range(4):
@@ -576,16 +557,14 @@
             row = cg_rows[0, 0:1, :] if j == 0 else cg_in[j, 0:1, :]
             answer += jnp.where(ids_ref[...] == jnp.bitwise_xor(ex, j), row, 0.0)
         cg_out[...] = answer
-        store(cg_out, cg_hbm)
 
     other_matmul(1)
-    pass_dy(0)
     pass_dy(1)
     other_pointwise(1)
+    down_part(0)
+    pass_dy(2)
     turned(256)
-    pass_dy(2)
     pass_dy(3)
-    down_part(0)
     down_part(1)
     hidden_part(256, True, 0, 512)
     pass_dy(4)
@@ -593,123 +572,121 @@
     down_part(3)
     pass_dy(5)
     hidden_part(256, False, 512, 512)
+    step1(d[0], 0)
     down_part(4)
     pass_dy(6)
-    step1(d[0], 0)
+    step1(d[1], 0)
     down_part(5)
     pass_dy(7)
-    step1(d[1], 0)
     hidden_part(256, False, 1024, 512)
+    step1(d[2], 0)
     down_part(6)
-    step1(d[2], 0)
     step1(d[3], 0)
     down_part(7)
     hidden_part(256, False, 1536, 512)
+    step1(d[0], 1)
+    backward(256)
+    step1(d[1], 1)
     step1(d[4], 0)
-    backward(256)
     far_first(0)
     step1(d[5], 0)
+    far_first(1)
     up_first(up[0])
+    step1(d[2], 1)
+    up_first(up[1])
     up_first(up[2])
+    step1(d[3], 1)
     up_first(up[3])
-    far_first(1)
     step1(d[6], 0)
-    step1(d[1], 1)
-    up_first(up[1])
     far_part(0, zh)
-    step1(d[3], 1)
-    up_rest(up[2])
-    step1(d[2], 1)
     step1(d[7], 0)
     far_part(1, zh)
+    step2(d[1], 0)
+    up_rest(up[0])
+    step1(d[4], 1)
+    step2(d[0], 0)
     up_rest(up[1])
     step1(d[5], 1)
+    step2(d[2], 0)
+    up_rest(up[2])
     up_rest(up[3])
+    step1(up[0], 0)
+    combine_part()
     row_part(1, 0)
-    combine_part()
+    step1(up[1], 0)
     row_part(1, 1)
+    far_sum(far[0])
+    row_part(1, 2)
+    step1(up[2], 0)
+    step2(d[3], 0)
+    row_part(1, 3)
     step1(up[3], 0)
-    row_part(1, 2)
-    far_sum(far[0])
-    row_part(1, 3)
-    step1(up[2], 0)
     row_part(0, 0)
-    step1(up[1], 0)
+    step1(d[6], 1)
+    step1(d[7], 1)
+    step2(d[1], 1)
     row_part(0, 1)
-    step2(d[1], 0)
-    step2(d[2], 0)
-    step2(d[3], 0)
+    step2(d[4], 0)
+    step2(d[0], 1)
     row_part(0, 2)
-    step1(d[7], 1)
     add_far()
     row_part(0, 3)
-    up_rest(up[0])
-    step1(up[0], 0)
-    step1(d[0], 1)
-    step1(d[4], 1)
-    step1(d[6], 1)
     far_sum(far[1])
     step2(d[5], 0)
+    step2(d[2], 1)
+    far_sum(far[2])
+    step1(up[0], 1)
     step1(far[0], 0)
+    step1(up[1], 1)
+    step1(up[3], 1)
+    step2(d[6], 0)
     step1(up[2], 1)
-    step2(d[1], 1)
     step2(d[3], 1)
-    far_sum(far[2])
+    step2(d[4], 1)
     step2(d[7], 0)
-    step1(up[3], 1)
-    step1(up[1], 1)
-    step2(d[2], 1)
-    step2(d[0], 0)
-    step2(d[4], 0)
-    step2(d[6], 0)
     far_sum(far[3])
-    step1(up[0], 1)
+    step2(d[5], 1)
+    result(d[1])
     step1(far[1], 0)
-    step2(d[5], 1)
+    result(d[0])
+    step1(far[2], 0)
+    step2(up[0], 0)
     step1(far[0], 1)
+    step2(d[6], 1)
+    step2(up[1], 0)
     step2(up[2], 0)
-    step1(far[2], 0)
-    step2(d[0], 1)
-    step2(d[7], 1)
-    step2(d[4], 1)
-    step2(d[6], 1)
     step2(up[3], 0)
     step1(far[3], 0)
-    step2(up[1], 0)
-    step2(up[0], 0)
+    step2(d[7], 1)
     step1(far[2], 1)
     step1(far[1], 1)
+    step2(up[0], 1)
+    step2(up[1], 1)
     step2(far[0], 0)
+    step2(up[2], 1)
     step2(up[3], 1)
-    step2(up[2], 1)
     step1(far[3], 1)
-    step2(up[1], 1)
-    add_rows()
-    step2(up[0], 1)
-    combine_result()
     step2(far[2], 0)
     step2(far[1], 0)
+    add_rows()
+    combine_result()
     step2(far[0], 1)
-    result(d[1])
-    result(d[3])
     result(d[2])
     step2(far[3], 0)
+    result(d[3])
+    result(d[4])
     result(d[5])
-    result(d[0])
-    result(d[7])
-    result(d[4])
-    result(d[6])
     step2(far[2], 1)
     step2(far[1], 1)
+    result(d[6])
+    result(d[7])
+    result(up[0])
+    result(up[1])
+    result(up[2])
+    step2(far[3], 1)
     result(up[3])
-    result(up[2])
-    result(up[1])
-    step2(far[3], 1)
-    result(up[0])
 
     wire.finish()
-    for store in stores:
-        store.wait()
 
 
 def hand_over(*refs):
@@ -731,9 +708,9 @@
     vmem = pl.BlockSpec(memory_space=pltpu.VMEM)
     outs = pl.pallas_call(
         kernel,
-        out_shape=OUTS,
+        out_shape=tuple(pltpu.VMEM(o.shape, o.dtype) for o in OUTS),
         in_specs=[hbm, hbm, vmem, vmem, hbm, hbm, hbm],
-        out_specs=(hbm, hbm, hbm, hbm, hbm),
+        out_specs=(vmem,) * 5,
         scratch_shapes=[
             pltpu.VMEM((D, FF), BF16),
             pltpu.VMEM((D, FF), BF16),
@@ -769,12 +746,7 @@
             pltpu.VMEM((8, 24, 256), BF16),
             pltpu.VMEM((4, 64, 256), BF16),
             pltpu.VMEM((4, 4, 4, 64, 128), BF16),
-            pltpu.VMEM((T, D), BF16),
-            pltpu.VMEM((2, T), F32),
-            pltpu.VMEM((1, 64, FF), BF16),
-            pltpu.VMEM((1, 64, FF), BF16),
-            pltpu.VMEM((1, 24, D), BF16),
-            pltpu.SemaphoreType.DMA((10,)),
+            pltpu.SemaphoreType.DMA((5,)),
             pltpu.SemaphoreType.DMA((N_SEM,)),
         ],
         compiler_params=pltpu.CompilerParams(
@@ -788,7 +760,7 @@
         in_specs=[vmem] * 5,
         out_specs=(vmem,) * 5,
         name="hand_over",
-    )(*outs)
+    )(*(pltpu.with_memory_space_constraint(o, pltpu.VMEM) for o in outs))
     return (outs[0], outs[1].T, *outs[2:])
 
 

time: 82.8 us -> 81.2 us (0.981)
  Pallas kernels: 82 us -> 80.4 us
    pallas_call x1, Pallas kernels: 2.03 us -> 0.94 us  [shards(): pl.pallas_call(hand_over, out_shape=OUTS, in_specs=[vmem] * 5, out_specs=...]
where the time goes in v4:
time: 81.2 us; the launch traced here: 81.1 us
  Pallas kernels  80.4 us (99%)
    pallas_call x1, Pallas kernels, shards(): pl.pallas_call(kernel, out_shape=tuple((pltpu.VMEM(o.shape, o.dtype) for...  79.5 us

profile of v4, /device:TPU:0, one launch (start us, length us, event | category | flops | bytes accessed | tf_op | source)
XLA Modules:
  0.0 81.1 jit_solution(8996271982408692109)
XLA Ops:
  0.6 79.5 %experts.1 = (bf16[128,2048]{1,0:T(8,128)(2,1)S(1)}, f32[2,128]{1,0:T(2,128)S(1)}, bf16[1,64,768]{2,1,0:T(8,128)(2,1)S(1)}, bf16[1,64,768]{2,1,0:T(8,128)(2,1)S(1)}, bf16[1,24,2048]{2,1,0:T(8,128)(2,1)S(1)}) custom-call(bf16[128,2048]{1,0:T(8,128)(2,1)} %x_hbm.1, bf16[128,2048]{1,0:T(8,128)(2,1)} %dy_hbm.1, s32[2,128]{1,0:T(2,128)} %bitcast.3, ...), custom_call_target="tpu_custom_call" | custom-call | tf_op jit(solution)/shard_map/experts/pallas_call | solution.py:709
  80.1 0.9 %hand_over.1 = (bf16[128,2048]{1,0:T(8,128)(2,1)}, f32[2,128]{1,0:T(2,128)}, bf16[1,64,768]{2,1,0:T(8,128)(2,1)}, bf16[1,64,768]{2,1,0:T(8,128)(2,1)}, bf16[1,24,2048]{2,1,0:T(8,128)(2,1)}) custom-call(bf16[128,2048]{1,0:T(8,128)(2,1)S(1)} %get-tuple-element.15.refs_0_, f32[2,128]{1,0:T(2,128)S(1)} %get-tuple-element.16.refs_1_, ...), custom_call_target="tpu_custom_call" | custom-call | tf_op jit(solution)/shard_map/hand_over/pallas_call | solution.py:757

commit v5 on v4

--- a/solution.py
+++ b/solution.py
@@ -11,7 +11,7 @@
 D = 2048
 FF = 768
 T = 128
-N_SEM = 150
+N_SEM = 132
 
 
 def mod4(v):
@@ -81,22 +81,28 @@
 
     def chunk(self, way, c):
         if self.far:
-            rows = pl.ds(32 * way, 32)
-            return (c, slice(None), rows) if self.first == "x" else (slice(None), c, rows)
+            x, y = (c, slice(None)) if self.first == "x" else (slice(None), c)
+            return (x, y, *self.share(way))
         return (c, way) if self.first == "x" else (slice(None), way, c)
+
+    def share(self, way):
+        rows, cols = self.recv1.shape[-2:]
+        if self.recv3.shape[-2] == rows:
+            return (slice(None), pl.ds(cols * way, cols))
+        return (pl.ds(rows * way, rows), slice(None))
 
     def own(self, way, c, j):
         x, y = (c, j) if self.first == "x" else (j, c)
         if self.far:
-            return self.recv3[x, y, 32 * way : 32 * way + 32]
+            return self.recv3[(x, y, *self.share(way))]
         return self.partial[x, way, y]
 
 
 def kernel(
     x_hbm,
     dy_hbm,
-    ids_ref,
-    comb_ref,
+    ids_hbm,
+    comb_hbm,
     wg_hbm,
     wu_hbm,
     wd_hbm,
@@ -139,6 +145,14 @@
     rd3,
     rg3,
     rz3,
+    rf1,
+    rf2,
+    rf3,
+    rn1,
+    rn2,
+    rn3,
+    ids_ref,
+    comb_ref,
     local_sem,
     remote_sem,
 ):
@@ -156,6 +170,10 @@
     z_near = {"dp": dp, "expert": (1 - zl) * 2 + core}
     z_diag = {"dp": dp, "expert": (1 - zl) * 2 + 1 - core}
 
+    small = [
+        pltpu.make_async_copy(ids_hbm, ids_ref, local_sem.at[5]),
+        pltpu.make_async_copy(comb_hbm, comb_ref, local_sem.at[6]),
+    ]
     loads = [
         pltpu.make_async_copy(x_hbm, x.at[pl.ds(0, T)], local_sem.at[0]),
         pltpu.make_async_copy(dy_hbm, dy.at[pl.ds(0, T)], local_sem.at[1]),
@@ -163,13 +181,19 @@
         pltpu.make_async_copy(wu_hbm.at[0], wu, local_sem.at[3]),
         pltpu.make_async_copy(wd_hbm.at[0], wd, local_sem.at[4]),
     ]
-    for load in loads:
-        load.start()
-
     barrier = pltpu.get_barrier_semaphore()
     peers = (x_next, x_prev, y_next, y_prev, z_far, mate, z_near, z_diag)
     for peer in peers:
         pl.semaphore_signal(barrier, inc=1, device_id=peer, device_id_type=MESH)
+    for load in small + loads:
+        load.start()
+    for load in small:
+        load.wait()
+    expert = lax.broadcasted_iota(jnp.int32, (8, T), 0)
+    dense = jnp.zeros((8, T), F32)
+    for k in range(2):
+        dense += jnp.where(ids_ref[k : k + 1, :] == expert, comb_ref[k : k + 1, :], 0.0)
+    weight_rows[0] = dense
     pl.semaphore_wait(barrier, len(peers))
 
     wire = Wire(remote_sem, mate)
@@ -191,11 +215,6 @@
     dy_pass_send, dy_diag = wire.group(slot_rows(dy, 2)), [wire.sem() for _ in range(8)]
     w_send, w_in = wire.group(weight_rows.at[pl.ds(1, 3)]), wire.sem()
 
-    expert = lax.broadcasted_iota(jnp.int32, (8, T), 0)
-    dense = jnp.zeros((8, T), F32)
-    for k in range(2):
-        dense += jnp.where(ids_ref[k : k + 1, :] == expert, comb_ref[k : k + 1, :], 0.0)
-    weight_rows[0] = dense
     for j, to in ((1, mate), (2, z_near), (3, z_diag)):
         wire.put(weight_rows.at[0], weight_rows.at[j], to, w_send, w_in)
 
@@ -257,7 +276,7 @@
             dact[:, cols] = nn(x[0:256, :], wu[:, cols])
             return carry
 
-        lax.fori_loop(0, FF // 256, matmul, 0)
+        lax.fori_loop(0, FF // 256, matmul, 0, unroll=True)
 
         def pointwise(i, carry):
             start = pl.multiple_of(i * 16, 16)
@@ -278,7 +297,7 @@
                 out[T + 64 * b : T + 64 * b + 64, cols] = r[64:128]
             return carry
 
-        lax.fori_loop(0, FF // 256, matmul, 0)
+        lax.fori_loop(0, FF // 256, matmul, 0, unroll=True)
 
     def other_pointwise(b):
         def pointwise(i, carry):
@@ -298,7 +317,7 @@
             hg[:, cols] = r if first else hg[:, cols] + r
             return carry
 
-        lax.fori_loop(0, FF // 256, matmul, 0)
+        lax.fori_loop(0, FF // 256, matmul, 0, unroll=True)
 
     def backward(r0):
         def pointwise(i, carry):
@@ -348,15 +367,19 @@
 
     d = [
         Stream(wire, axis(j), pd.at[j], rd1.at[j], rd2.at[j], rd3.at[j], d_sends, down, 256 * j)
-        for j in range(8)
+        for j in range(7)
     ]
+    far_sends = [wire.group(ref) for ref in (rf1, rf2, rf3)]
+    far_down = Stream(wire, "x", pd.at[7], rf1, rf2, rf3, far_sends, down, 1792, True)
+    narrow_sends = [wire.group(ref) for ref in (rn1, rn2, rn3)]
+    narrow = Stream(wire, "y", pz.at[3], rn1, rn2, rn3, narrow_sends, upper, 640)
     up = [
         Stream(wire, axis(j), pg.at[j], rg1.at[j], rg2.at[j], rg3.at[j], g_sends, sums, 256 * (j % 2))
         for j, sums in enumerate((gate, gate, upper, upper))
     ]
     far = [
         Stream(wire, axis(j), pz.at[j], rz1.at[j], rz2.at[j], rz3.at[j], z_sends, sums, c0, True)
-        for j, (sums, c0) in enumerate(((gate, 512), (gate, 640), (upper, 512), (upper, 640)))
+        for j, (sums, c0) in enumerate(((gate, 512), (gate, 640), (upper, 512)))
     ]
 
     def ring(first, way):
@@ -386,7 +409,10 @@
         wire.arrived(dy_block(3, j), dy_diag[j])
         r = nn(hct[...], dy[:, 256 * j : 256 * j + 256]).reshape(4, 2, 4, 24, 256)
         pd[j] = r.astype(BF16)
-        launch(d[j])
+        if j < 7:
+            launch(d[j])
+        else:
+            wire.put(pd.at[7, :, 1 - zh], rf3, z_far, far_down.send3, far_down.sem3)
 
     def up_chunk(st, away):
         right, c0 = st.sums.right, st.c0
@@ -428,7 +454,7 @@
             pz[k + 1, c, half] = r[:, :, 128:256]
             return carry
 
-        lax.fori_loop(0, 4, body, 0)
+        lax.fori_loop(0, 4, body, 0, unroll=True)
 
     def far_first(kind):
         far_part(kind, 1 - zh)
@@ -487,7 +513,11 @@
                 continue
             total += st.recv2[way, 2].astype(F32)
             if st.far:
-                st.sums.put(slice(32 * way, 32 * way + 32), st.c0, total)
+                rows, cols = total.shape
+                if st.recv3.shape[-2] == rows:
+                    st.sums.put(slice(None), st.c0 + cols * way, total)
+                else:
+                    st.sums.put(slice(rows * way, rows * way + rows), st.c0, total)
             else:
                 st.recv2[way, 2] = total.astype(BF16)
         if s == 1 and not st.far:
@@ -511,7 +541,7 @@
             rg[r0 : r0 + 256, cols] = r.astype(BF16)
             return carry
 
-        lax.fori_loop(0, 2, body, 0)
+        lax.fori_loop(0, 2, body, 0, unroll=True)
         if q == 3:
             if half == 1:
                 wire.put(slot_rows(rg, 3), rc.at[1], mate, rc_send, rc_far)
@@ -566,15 +596,15 @@
     turned(256)
     pass_dy(3)
     down_part(1)
-    hidden_part(256, True, 0, 512)
+    down_part(2)
     pass_dy(4)
-    down_part(2)
     down_part(3)
     pass_dy(5)
+    hidden_part(256, True, 0, 512)
+    step1(d[0], 0)
     hidden_part(256, False, 512, 512)
-    step1(d[0], 0)
+    pass_dy(6)
     down_part(4)
-    pass_dy(6)
     step1(d[1], 0)
     down_part(5)
     pass_dy(7)
@@ -583,108 +613,110 @@
     down_part(6)
     step1(d[3], 0)
     down_part(7)
+    step1(d[0], 1)
     hidden_part(256, False, 1536, 512)
-    step1(d[0], 1)
     backward(256)
-    step1(d[1], 1)
     step1(d[4], 0)
+    up_first(up[0])
     far_first(0)
     step1(d[5], 0)
     far_first(1)
-    up_first(up[0])
-    step1(d[2], 1)
     up_first(up[1])
     up_first(up[2])
+    up_first(up[3])
+    step1(d[1], 1)
+    step1(d[2], 1)
+    far_part(0, zh)
+    far_part(1, zh)
+    launch_relay(narrow)
+    step2(d[0], 0)
+    launch_direct(narrow)
+    up_rest(up[1])
+    step1(d[4], 1)
+    up_rest(up[3])
+    step1(d[6], 0)
+    up_rest(up[2])
+    far_sum(far_down)
     step1(d[3], 1)
-    up_first(up[3])
-    step1(d[6], 0)
-    far_part(0, zh)
-    step1(d[7], 0)
-    far_part(1, zh)
-    step2(d[1], 0)
-    up_rest(up[0])
-    step1(d[4], 1)
-    step2(d[0], 0)
-    up_rest(up[1])
-    step1(d[5], 1)
-    step2(d[2], 0)
-    up_rest(up[2])
-    up_rest(up[3])
-    step1(up[0], 0)
     combine_part()
     row_part(1, 0)
     step1(up[1], 0)
     row_part(1, 1)
-    far_sum(far[0])
     row_part(1, 2)
     step1(up[2], 0)
+    step2(d[1], 0)
+    step1(up[3], 0)
+    step1(d[6], 1)
+    far_sum(far[0])
+    up_rest(up[0])
+    step1(up[0], 0)
+    step1(narrow, 0)
+    step2(d[0], 1)
+    step1(d[5], 1)
+    step2(d[2], 0)
+    step1(far_down, 0)
+    row_part(1, 3)
+    step2(d[4], 0)
+    row_part(0, 0)
+    row_part(0, 1)
+    far_sum(far[1])
+    step1(up[2], 1)
+    row_part(0, 2)
+    step2(d[1], 1)
+    row_part(0, 3)
+    add_far()
+    step1(far[0], 0)
     step2(d[3], 0)
-    row_part(1, 3)
-    step1(up[3], 0)
-    row_part(0, 0)
-    step1(d[6], 1)
-    step1(d[7], 1)
-    step2(d[1], 1)
-    row_part(0, 1)
-    step2(d[4], 0)
-    step2(d[0], 1)
-    row_part(0, 2)
-    add_far()
-    row_part(0, 3)
-    far_sum(far[1])
+    far_sum(far[2])
+    step1(up[3], 1)
+    step1(up[0], 1)
     step2(d[5], 0)
+    step2(d[6], 0)
+    step1(far_down, 1)
+    step1(up[1], 1)
+    result(d[1])
+    step1(narrow, 1)
+    step1(far[0], 1)
     step2(d[2], 1)
-    far_sum(far[2])
-    step1(up[0], 1)
-    step1(far[0], 0)
-    step1(up[1], 1)
-    step1(up[3], 1)
-    step2(d[6], 0)
-    step1(up[2], 1)
     step2(d[3], 1)
+    step1(far[2], 0)
+    step1(far[1], 0)
+    step2(up[3], 0)
+    step2(up[2], 0)
+    step2(d[5], 1)
+    step2(up[0], 0)
+    step2(up[1], 0)
     step2(d[4], 1)
-    step2(d[7], 0)
-    far_sum(far[3])
-    step2(d[5], 1)
-    result(d[1])
-    step1(far[1], 0)
-    result(d[0])
-    step1(far[2], 0)
-    step2(up[0], 0)
-    step1(far[0], 1)
     step2(d[6], 1)
-    step2(up[1], 0)
-    step2(up[2], 0)
-    step2(up[3], 0)
-    step1(far[3], 0)
-    step2(d[7], 1)
+    step2(narrow, 0)
+    step2(far[0], 0)
     step1(far[2], 1)
     step1(far[1], 1)
+    step2(up[3], 1)
+    step2(up[2], 1)
+    step2(far_down, 0)
     step2(up[0], 1)
+    add_rows()
     step2(up[1], 1)
-    step2(far[0], 0)
-    step2(up[2], 1)
-    step2(up[3], 1)
-    step1(far[3], 1)
+    result(d[2])
+    combine_result()
+    result(d[3])
+    result(d[5])
+    step2(narrow, 1)
+    step2(far[0], 1)
+    result(d[4])
+    result(d[6])
     step2(far[2], 0)
     step2(far[1], 0)
-    add_rows()
-    combine_result()
-    step2(far[0], 1)
-    result(d[2])
-    step2(far[3], 0)
-    result(d[3])
-    result(d[4])
-    result(d[5])
+    result(d[0])
+    result(up[3])
+    step2(far_down, 1)
+    result(up[0])
     step2(far[2], 1)
     step2(far[1], 1)
-    result(d[6])
-    result(d[7])
-    result(up[0])
     result(up[1])
     result(up[2])
-    step2(far[3], 1)
-    result(up[3])
+    result(narrow)
 
     wire.finish()
 
@@ -709,7 +741,7 @@
     outs = pl.pallas_call(
         kernel,
         out_shape=tuple(pltpu.VMEM(o.shape, o.dtype) for o in OUTS),
-        in_specs=[hbm, hbm, vmem, vmem, hbm, hbm, hbm],
+        in_specs=[hbm] * 7,
         out_specs=(vmem,) * 5,
         scratch_shapes=[
             pltpu.VMEM((D, FF), BF16),
@@ -737,16 +769,24 @@
             pltpu.VMEM((8, 4, 2, 4, 24, 256), BF16),
             pltpu.VMEM((4, 4, 2, 4, 64, 256), BF16),
             pltpu.VMEM((4, 4, 2, 4, 64, 128), BF16),
-            pltpu.VMEM((8, 2, 3, 4, 24, 256), BF16),
+            pltpu.VMEM((7, 2, 3, 4, 24, 256), BF16),
             pltpu.VMEM((4, 2, 3, 4, 64, 256), BF16),
-            pltpu.VMEM((4, 2, 3, 4, 32, 128), BF16),
-            pltpu.VMEM((8, 2, 3, 24, 256), BF16),
+            pltpu.VMEM((3, 2, 3, 4, 32, 128), BF16),
+            pltpu.VMEM((7, 2, 3, 24, 256), BF16),
             pltpu.VMEM((4, 2, 3, 64, 256), BF16),
-            pltpu.VMEM((4, 2, 3, 32, 128), BF16),
-            pltpu.VMEM((8, 24, 256), BF16),
+            pltpu.VMEM((3, 2, 3, 32, 128), BF16),
+            pltpu.VMEM((7, 24, 256), BF16),
             pltpu.VMEM((4, 64, 256), BF16),
-            pltpu.VMEM((4, 4, 4, 64, 128), BF16),
-            pltpu.SemaphoreType.DMA((5,)),
+            pltpu.VMEM((3, 4, 4, 64, 128), BF16),
+            pltpu.VMEM((2, 3, 4, 24, 128), BF16),
+            pltpu.VMEM((2, 3, 24, 128), BF16),
+            pltpu.VMEM((4, 4, 24, 256), BF16),
+            pltpu.VMEM((2, 3, 4, 64, 128), BF16),
+            pltpu.VMEM((2, 3, 64, 128), BF16),
+            pltpu.VMEM((64, 128), BF16),
+            pltpu.VMEM((2, T), jnp.int32),
+            pltpu.VMEM((2, T), F32),
+            pltpu.SemaphoreType.DMA((7,)),
             pltpu.SemaphoreType.DMA((N_SEM,)),
         ],
         compiler_params=pltpu.CompilerParams(

time: 81.2 us -> 78.3 us (0.964)
  Pallas kernels: 80.4 us -> 77.6 us
    pallas_call x1, Pallas kernels: 79.5 us -> 76.6 us  [shards(): pl.pallas_call(kernel, out_shape=tuple((pltpu.VMEM(o.shape, o.dtype) for...]
where the time goes in v5:
time: 78.3 us; the launch traced here: 78.2 us
  Pallas kernels  77.6 us (99%)
    pallas_call x1, Pallas kernels, shards(): pl.pallas_call(kernel, out_shape=tuple((pltpu.VMEM(o.shape, o.dtype) for...  76.6 us

profile of v5, /device:TPU:0, one launch (start us, length us, event | category | flops | bytes accessed | tf_op | source)
XLA Modules:
  0.0 78.2 jit_solution(3870158090376323385)
XLA Ops:
  0.6 76.6 %experts.1 = (bf16[128,2048]{1,0:T(8,128)(2,1)S(1)}, f32[2,128]{1,0:T(2,128)S(1)}, bf16[1,64,768]{2,1,0:T(8,128)(2,1)S(1)}, bf16[1,64,768]{2,1,0:T(8,128)(2,1)S(1)}, bf16[1,24,2048]{2,1,0:T(8,128)(2,1)S(1)}) custom-call(bf16[128,2048]{1,0:T(8,128)(2,1)} %x_hbm.1, bf16[128,2048]{1,0:T(8,128)(2,1)} %dy_hbm.1, s32[2,128]{1,0:T(2,128)} %bitcast.3, ...), custom_call_target="tpu_custom_call" | custom-call | tf_op jit(solution)/shard_map/experts/pallas_call | solution.py:741
  77.3 0.9 %hand_over.1 = (bf16[128,2048]{1,0:T(8,128)(2,1)}, f32[2,128]{1,0:T(2,128)}, bf16[1,64,768]{2,1,0:T(8,128)(2,1)}, bf16[1,64,768]{2,1,0:T(8,128)(2,1)}, bf16[1,24,2048]{2,1,0:T(8,128)(2,1)}) custom-call(bf16[128,2048]{1,0:T(8,128)(2,1)S(1)} %get-tuple-element.15.refs_0_, f32[2,128]{1,0:T(2,128)S(1)} %get-tuple-element.16.refs_1_, ...), custom_call_target="tpu_custom_call" | custom-call | tf_op jit(solution)/shard_map/hand_over/pallas_call | solution.py:797

commit v6 on v5

--- a/solution.py
+++ b/solution.py
@@ -185,7 +185,7 @@
     peers = (x_next, x_prev, y_next, y_prev, z_far, mate, z_near, z_diag)
     for peer in peers:
         pl.semaphore_signal(barrier, inc=1, device_id=peer, device_id_type=MESH)
-    for load in small + loads:
+    for load in loads[0:1] + small + loads[1:2]:
         load.start()
     for load in small:
         load.wait()
@@ -215,13 +215,14 @@
     dy_pass_send, dy_diag = wire.group(slot_rows(dy, 2)), [wire.sem() for _ in range(8)]
     w_send, w_in = wire.group(weight_rows.at[pl.ds(1, 3)]), wire.sem()
 
+    loads[0].wait()
     for j, to in ((1, mate), (2, z_near), (3, z_diag)):
         wire.put(weight_rows.at[0], weight_rows.at[j], to, w_send, w_in)
-
-    loads[0].wait()
     for j in range(2):
         wire.put(x_block(0, j), x_block(2, j), z_near, x_near_send, x_near[j])
     wire.put(slot_rows(x, 0), slot_rows(x, 1), mate, x_mate_send, x_mate)
+    for load in loads[2:5]:
+        load.start()
     loads[1].wait()
     for j in range(8):
         wire.put(dy_block(0, j), dy_block(2, j), z_near, dy_near_send, dy_near[j])

time: 78.3 us -> 78.3 us (level)
  no operation moved by 1% of the time
where the time goes in v6:
time: 78.3 us; the launch traced here: 78.2 us
  Pallas kernels  77.6 us (99%)
    pallas_call x1, Pallas kernels, shards(): pl.pallas_call(kernel, out_shape=tuple((pltpu.VMEM(o.shape, o.dtype) for...  76.6 us

profile of v6, /device:TPU:0, one launch (start us, length us, event | category | flops | bytes accessed | tf_op | source)
XLA Modules:
  0.0 78.2 jit_solution(12503615448419639797)
XLA Ops:
  0.6 76.6 %experts.1 = (bf16[128,2048]{1,0:T(8,128)(2,1)S(1)}, f32[2,128]{1,0:T(2,128)S(1)}, bf16[1,64,768]{2,1,0:T(8,128)(2,1)S(1)}, bf16[1,64,768]{2,1,0:T(8,128)(2,1)S(1)}, bf16[1,24,2048]{2,1,0:T(8,128)(2,1)S(1)}) custom-call(bf16[128,2048]{1,0:T(8,128)(2,1)} %x_hbm.1, bf16[128,2048]{1,0:T(8,128)(2,1)} %dy_hbm.1, s32[2,128]{1,0:T(2,128)} %bitcast.3, ...), custom_call_target="tpu_custom_call" | custom-call | tf_op jit(solution)/shard_map/experts/pallas_call | solution.py:742
  77.3 0.9 %hand_over.1 = (bf16[128,2048]{1,0:T(8,128)(2,1)}, f32[2,128]{1,0:T(2,128)}, bf16[1,64,768]{2,1,0:T(8,128)(2,1)}, bf16[1,64,768]{2,1,0:T(8,128)(2,1)}, bf16[1,24,2048]{2,1,0:T(8,128)(2,1)}) custom-call(bf16[128,2048]{1,0:T(8,128)(2,1)S(1)} %get-tuple-element.15.refs_0_, f32[2,128]{1,0:T(2,128)S(1)} %get-tuple-element.16.refs_1_, ...), custom_call_target="tpu_custom_call" | custom-call | tf_op jit(solution)/shard_map/hand_over/pallas_call | solution.py:798
